TPU v7x, 32 devices: a whole 2x2x4 slice. The times are simulated.
32 devices in a mesh: rep: 2 (over x), ctx: 16 (over z, y, core).
Axes of the slice: x: 2, y: 2, z: 4, core: 2. Of those that a mesh axis runs over, the one named last changes fastest.
Arguments:
- queries: bfloat16 [4096, 32, 128], P(('rep', 'ctx')), parts along dimension 0, may hold values from -128 to 128
- keys: bfloat16 [4096, 2, 128], P(('rep', 'ctx')), parts along dimension 0, may hold values from -5 to 5
- values: bfloat16 [4096, 2, 128], P(('rep', 'ctx')), parts along dimension 0, may hold values from -6 to 6
- grad_out: bfloat16 [4096, 32, 128], P(('rep', 'ctx')), parts along dimension 0, may hold values from -6 to 6
- selected: int32 [4096, 2, 8], P(('rep', 'ctx')), parts along dimension 0, may hold values from 0 to 31, as said below
Outputs:
- dquery: bfloat16 [4096, 32, 128], P(('rep', 'ctx')), parts along dimension 0
- key_grad: bfloat16 [4096, 2, 128], P(('rep', 'ctx')), parts along dimension 0
- value_grad: bfloat16 [4096, 2, 128], P(('rep', 'ctx')), parts along dimension 0
There are 2 independent parts, one for each index of `rep`. A program takes and returns all parts, laid end to end along the dimension named above; each array names one. Nothing has to cross between parts.
Inputs may be any that keep to these rules, and one draw needn't show every extreme that they name: The 8 blocks of selected[t, g] are different and include block t // 64 and block 0. Over the 128 tokens of one device of ctx, the blocks named for one group that lie on other devices number exactly 7, at most one of each other device; block 0 is among them for every device but the first.
All inputs are finite; a program needn't handle non-finite values.
Results may differ from a plain program's by a relative error of at most 0.0075.
Values may be sent and summed in bfloat16 or wider, within the bound.
A program may use at most 128 MiB of HBM per device.

v0:
```python
import functools
import math

import jax
import jax.numpy as jnp
from jax import lax
from jax.experimental import pallas as pl
from jax.experimental.pallas import tpu as pltpu
from jax.sharding import PartitionSpec as P

BLK = 64
NEG = -1e30
ID_ROWS = 16
LANES = 128
LOG2E = math.log2(math.e)
NT = (((1,), (1,)), ((), ()))
NN = (((1,), (0,)), ((), ()))


def attend(
    g, per_group, chunk_tokens, lo, hi, picked_ref, q_ref, do_ref, dq_ref, pool_ref, acc_ref
):
    tokens, _, dh = q_ref.shape
    own_rows = tokens
    keys = pool_ref.shape[1]
    slots = keys // BLK
    own_slots = own_rows // BLK
    scaling = 1.0 / math.sqrt(dh)
    log_scale = scaling * LOG2E
    rows = chunk_tokens * per_group
    shift = per_group.bit_length() - 1
    pool_k = pool_ref[0]
    pool_v = pool_ref[1]
    pool_kt = pool_k.T
    heads = slice(g * per_group, (g + 1) * per_group)

    @pl.loop(lo, hi)
    def _(c):
        t0 = pl.multiple_of(c * chunk_tokens, chunk_tokens)
        q = q_ref[pl.ds(t0, chunk_tokens), heads, :].reshape(rows, dh)
        do = do_ref[pl.ds(t0, chunk_tokens), heads, :].reshape(rows, dh)
        row_tok = t0 + (lax.broadcasted_iota(jnp.int32, (tokens, rows), 1) >> shift)
        tok = lax.broadcasted_iota(jnp.int32, (tokens, rows), 0)
        spread = jnp.where(row_tok == tok, 1.0, 0.0).astype(jnp.bfloat16)
        seen = lax.dot_general(picked_ref[g], spread, NN, preferred_element_type=jnp.float32)
        bias = (seen - 1.0) * (-NEG)
        s = lax.dot_general(pool_k, q, NT, preferred_element_type=jnp.float32)
        dp = lax.dot_general(pool_v, do, NT, preferred_element_type=jnp.float32)
        pieces = []
        for j in range(slots):
            piece = s[j * BLK : (j + 1) * BLK] + bias[j : j + 1]
            if j < own_slots:
                key_pos = j * BLK + lax.broadcasted_iota(jnp.int32, (BLK, rows), 0)
                causal = key_pos <= row_tok[:BLK]
                piece = jnp.where(causal, piece, NEG)
            pieces.append(piece)
        s = jnp.concatenate(pieces, axis=0)
        peak = jnp.max(s, axis=0, keepdims=True)
        e = jnp.exp2((s - peak) * log_scale)
        total = jnp.sum(e, axis=0, keepdims=True)
        weighted = jnp.sum(e * dp, axis=0, keepdims=True)
        inv = 1.0 / total
        inner = weighted * inv
        p = e * inv
        ds = (p * (dp - inner)).astype(jnp.bfloat16)
        p = p.astype(jnp.bfloat16)
        dqt = lax.dot_general(pool_kt, ds, NN, preferred_element_type=jnp.float32)
        dq = (dqt * scaling).T.astype(jnp.bfloat16)
        dq_ref[pl.ds(t0, chunk_tokens), heads, :] = dq.reshape(chunk_tokens, per_group, dh)
        dk = lax.dot_general(ds, q, NN, preferred_element_type=jnp.float32)
        dv = lax.dot_general(p, do, NN, preferred_element_type=jnp.float32)
        acc_ref[0] += dk.reshape(slots, BLK, dh)
        acc_ref[1] += dv.reshape(slots, BLK, dh)


def fill_tables(g, n, me, n_far, own_blocks, sel_ref, picked_ref, tab_ref):
    sel = sel_ref[g]
    tokens = sel.shape[1]
    shift = own_blocks.bit_length() - 1
    owner = sel >> shift
    block = sel & (own_blocks - 1)
    peers = lax.broadcasted_iota(jnp.int32, (n, tokens), 0)
    code = jnp.zeros((n, tokens), jnp.float32)
    for i in range(sel.shape[0]):
        mark = (block[i : i + 1] + 1).astype(jnp.float32)
        code = jnp.maximum(code, jnp.where(owner[i : i + 1] == peers, mark, 0.0))
    code = jnp.broadcast_to(jnp.max(code, axis=1, keepdims=True), (n, LANES))
    peers = lax.broadcasted_iota(jnp.int32, (n, LANES), 0)
    code = jnp.where(peers == me, 0.0, code)
    live = jnp.where(code > 0.0, 1.0, 0.0)
    before = lax.broadcasted_iota(jnp.int32, (n, n), 1) < lax.broadcasted_iota(jnp.int32, (n, n), 0)
    before = jnp.where(before, 1.0, 0.0).astype(jnp.bfloat16)
    slot = lax.dot_general(before, live.astype(jnp.bfloat16), NN, preferred_element_type=jnp.float32)
    far = jnp.maximum(code - 1.0, 0.0)
    lane = lax.broadcasted_iota(jnp.int32, (n, LANES), 1)
    kept = jnp.minimum(slot, float(n_far - 1))
    entry = jnp.where(lane == 0, kept, jnp.where(lane == 1, live, far))
    tab_ref[g, :n, :] = entry.astype(jnp.int32)
    peer = peers.astype(jnp.float32)
    now = me * own_blocks + (lax.broadcasted_iota(jnp.int32, (1, tokens), 1) >> BLK.bit_length() - 1)
    slots = picked_ref.shape[1]
    row = lax.broadcasted_iota(jnp.int32, (slots, tokens), 0)
    far_rows = tab_ref.shape[1] - n
    far_row = lax.broadcasted_iota(jnp.int32, (far_rows, LANES), 0)
    far_lane = lax.broadcasted_iota(jnp.int32, (far_rows, LANES), 1)
    far_entry = jnp.zeros((far_rows, LANES), jnp.float32)
    picked = jnp.zeros((slots, tokens), jnp.float32)
    for i in range(own_blocks + n_far):
        if i < own_blocks:
            ids = jnp.full((1, tokens), me * own_blocks + i, jnp.int32)
        else:
            hit = (live > 0.0) & (slot == float(i - own_blocks))
            who = jnp.max(jnp.where(hit, peer, -1.0), axis=0, keepdims=True)
            which = jnp.max(jnp.where(hit, far, 0.0), axis=0, keepdims=True)
            ids = jnp.max(who * own_blocks + which, axis=1, keepdims=True).astype(jnp.int32)
            ids = jnp.broadcast_to(ids, (1, tokens))
            here = jnp.where(far_lane == 0, jnp.maximum(who, 0.0), which)
            far_entry = jnp.where(far_row == i - own_blocks, here, far_entry)
        seen = jnp.max(jnp.where(sel == ids, 1.0, 0.0), axis=0, keepdims=True)
        seen = jnp.where(ids <= now, seen, 0.0)
        picked = jnp.where(row == i, seen, picked)
    tab_ref[g, n:, :] = far_entry.astype(jnp.int32)
    picked_ref[g] = picked.astype(jnp.bfloat16)


def fill_pool(g, n, n_far, tab, own_kv, gathered_ref, pool_ref):
    own_rows = own_kv.shape[2] * BLK
    pool_ref[:, :own_rows, :] = own_kv[g].reshape(2, own_rows, own_kv.shape[4])
    for s in range(n_far):
        owner = jnp.clip(tab[g, n + s, 0], 0, n - 1)
        block = jnp.clip(tab[g, n + s, 1], 0, own_kv.shape[2] - 1)
        lo = own_rows + s * BLK
        for kv in range(2):
            pool_ref[kv, lo : lo + BLK, :] = gathered_ref[owner, kv, block]


def fused_kernel(
    n, cols, n_far, chunk_tokens, groups,
    sel_ref, q_hbm, do_hbm, own_kv, dq_ref, key_out, value_out, *scratch,
):
    per_bank = 9
    banks = [scratch[g * per_bank : (g + 1) * per_bank] for g in range(groups)]
    (
        picked_ref, tab_ref, tab, q_ref, do_ref, mix_ref, in_sem, pool_ref, mid_ref, col_send, y_send, sib_send, recv_sem,
        rs_sem, ry_send, ry_recv, rz_send, rz_recv,
    ) = scratch[groups * per_bank :]
    depth = n // (2 * cols)
    chips = n // 2
    me = lax.axis_index("ctx")
    core = lax.rem(me, 2)
    chip = me // 2
    y = lax.rem(chip, cols)
    z = chip // cols
    sib = 2 * chip + 1 - core
    other_y = cols - 1 - y
    y_peer = 2 * (z * cols + other_y) + core
    own_blocks = own_kv.shape[2]
    own_rows = own_blocks * BLK
    dh = own_kv.shape[4]
    per_group = q_ref.shape[1] // groups
    chunks = q_ref.shape[0] // chunk_tokens
    scaling = 1.0 / math.sqrt(dh)

    def device(zz, yy, cc):
        return 2 * (zz * cols + yy) + cc

    def remote(src, dst, send, recv, peer):
        return pltpu.make_async_remote_copy(
            src_ref=src,
            dst_ref=dst,
            send_sem=send,
            recv_sem=recv,
            device_id={"ctx": peer},
            device_id_type=pl.DeviceIdType.MESH,
        )

    def col_copy(g, k):
        peer = device(lax.rem(z + k, depth), y, core)
        return remote(
            own_kv.at[g], banks[g][0].at[me], col_send.at[g, k], recv_sem.at[g, me], peer
        )

    def own_copy(g, sem, peer):
        return remote(own_kv.at[g], banks[g][0].at[me], sem, recv_sem.at[g, me], peer)

    def pass_on(g, src, sem, peer):
        slot = banks[g][0].at[src]
        return remote(slot, slot, sem, recv_sem.at[g, src], peer)

    def await_piece(g, src):
        pass_on(g, src, sib_send.at[g, src], sib).wait_recv()

    def gather_start(g):
        if cols > 1:
            own_copy(g, y_send.at[g, z], y_peer).start()

        @pl.loop(1, depth)
        def _(k):
            col_copy(g, k).start()

        own_copy(g, sib_send.at[g, me], sib).start()

    def gather_column(g):
        @pl.loop(1, depth)
        def _(k):
            from_z = lax.rem(z + depth - k, depth)
            src = device(from_z, y, core)
            await_piece(g, src)
            if cols > 1:
                pass_on(g, src, y_send.at[g, from_z], y_peer).start()
            pass_on(g, src, sib_send.at[g, src], sib).start()

    def gather_across(g):
        if cols > 1:
            @pl.loop(0, depth)
            def _(k):
                src = device(lax.rem(z + depth - k, depth), other_y, core)
                await_piece(g, src)
                pass_on(g, src, sib_send.at[g, src], sib).start()

    def gather_end(g):
        @pl.loop(0, chips)
        def _(q):
            await_piece(g, 2 * q + 1 - core)

    def gather_drain(g):
        @pl.loop(1, depth)
        def _(k):
            col_copy(g, k).wait_send()

        if cols > 1:
            @pl.loop(0, depth)
            def _(k):
                pass_on(g, device(k, y, core), y_send.at[g, k], y_peer).wait_send()

        @pl.loop(0, chips)
        def _(q):
            src = 2 * q + core
            pass_on(g, src, sib_send.at[g, src], sib).wait_send()

    def sib_copy(g):
        return remote(banks[g][2], banks[g][3], rs_sem.at[g, 0], rs_sem.at[g, 1], sib)

    def y_copy(g, k):
        return remote(
            banks[g][4].at[k], banks[g][5].at[k], ry_send.at[g, k], ry_recv.at[g, k], y_peer
        )

    def z_copy(g, to_z):
        peer = device(to_z, y, core)
        return remote(
            banks[g][6].at[to_z], banks[g][7].at[z], rz_send.at[g, to_z], rz_recv.at[g, z], peer
        )

    def z_arrival(g, from_z):
        peer = device(from_z, y, core)
        return remote(
            banks[g][6].at[from_z], banks[g][7].at[from_z],
            rz_send.at[g, from_z], rz_recv.at[g, from_z], peer,
        )

    def far_part(g, dest, kv):
        return banks[g][1][kv, own_blocks + jnp.clip(tab[g, dest, 0], 0, n_far - 1)]

    def return_start(g):
        acc_ref, box = banks[g][1], banks[g][2]
        acc_ref[0] = acc_ref[0] * scaling

        @pl.loop(0, chips)
        def _(q):
            dest = 2 * q + 1 - core
            keep = tab[g, dest, 1].astype(jnp.float32)
            ids = jnp.full((ID_ROWS, dh), tab[g, dest, 2].astype(jnp.float32), jnp.float32)
            box[q, :ID_ROWS, :] = ids.astype(jnp.bfloat16)
            for kv in range(2):
                lo = ID_ROWS + kv * BLK
                box[q, lo : lo + BLK, :] = (far_part(g, dest, kv) * keep).astype(jnp.bfloat16)

        sib_copy(g).start()

    def merged(g, zz, yy):
        q = zz * cols + yy
        dest = 2 * q + core
        box = banks[g][3]
        which = box[q, :ID_ROWS, :].astype(jnp.float32)[:1]
        keep = tab[g, dest, 1].astype(jnp.float32)
        block = jnp.full((1, dh), tab[g, dest, 2].astype(jnp.float32), jnp.float32)
        for kv in range(2):
            lo = ID_ROWS + kv * BLK
            theirs = box[q, lo : lo + BLK, :].astype(jnp.float32)
            mine = far_part(g, dest, kv) * keep
            for b in range(own_blocks):
                yield kv, b, (
                    jnp.where(block == float(b), mine, 0.0)
                    + jnp.where(which == float(b), theirs, 0.0)
                )

    def return_across(g):
        sib_copy(g).wait_recv()
        if cols > 1:
            @pl.loop(0, depth)
            def _(k):
                zz = lax.rem(z + 1 + k, depth)
                for kv, b, part in merged(g, zz, other_y):
                    banks[g][4][zz, kv, b] = part.astype(jnp.bfloat16)
                y_copy(g, zz).start()

        @pl.loop(0, depth)
        def _(k):
            for kv, b, part in merged(g, k, y):
                mid_ref[k, kv, b] = part

    def return_column(g):
        @pl.loop(1, depth)
        def _(k):
            to_z = lax.rem(z + k, depth)
            total = mid_ref[to_z]
            if cols > 1:
                y_copy(g, to_z).wait_recv()
                total = total + banks[g][5][to_z].astype(jnp.float32)
            banks[g][6][to_z] = total.astype(jnp.bfloat16)
            z_copy(g, to_z).start()

        total = mid_ref[z] + banks[g][1][:, :own_blocks]
        if cols > 1:
            y_copy(g, z).wait_recv()
            total = total + banks[g][5][z].astype(jnp.float32)
        banks[g][8][...] = total

    def return_end(g):
        @pl.loop(1, depth)
        def _(k):
            from_z = lax.rem(z + depth - k, depth)
            z_arrival(g, from_z).wait_recv()
            banks[g][8][...] += banks[g][7][from_z].astype(jnp.float32)

        for kv in range(2):
            whole = banks[g][8][kv].reshape(own_rows, dh)
            mix_ref[kv, pl.ds(g, own_rows, stride=groups), :] = whole

    def return_drain(g):
        sib_copy(g).wait_send()
        if cols > 1:
            @pl.loop(0, depth)
            def _(k):
                y_copy(g, k).wait_send()

        @pl.loop(1, depth)
        def _(k):
            z_copy(g, lax.rem(z + k, depth)).wait_send()

    barrier = pltpu.get_barrier_semaphore()

    def greet(peer):
        pl.semaphore_signal(
            barrier, inc=1, device_id={"ctx": peer}, device_id_type=pl.DeviceIdType.MESH
        )

    @pl.loop(1, depth)
    def _(k):
        greet(device(lax.rem(z + k, depth), y, core))

    if cols > 1:
        greet(y_peer)
    greet(sib)
    loads = [
        pltpu.make_async_copy(q_hbm, q_ref, in_sem.at[0]),
        pltpu.make_async_copy(do_hbm, do_ref, in_sem.at[1]),
    ]
    for load in loads:
        load.start()
    pl.semaphore_wait(barrier, depth + cols - 1)
    for g in range(groups):
        gather_start(g)
    for g in range(groups):
        fill_tables(g, n, me, n_far, own_blocks, sel_ref, picked_ref, tab_ref)
    to_scalars = pltpu.make_async_copy(tab_ref, tab, in_sem.at[2])
    to_scalars.start()
    for g in range(groups):
        banks[g][1][...] = jnp.zeros_like(banks[g][1])
    to_scalars.wait()
    for load in loads:
        load.wait()
    gather_column(0)
    gather_across(0)
    gather_end(0)
    for g in range(groups):
        first, last = [], []
        if g + 1 < groups:
            first.append(functools.partial(gather_column, g + 1))
            last.append(functools.partial(gather_across, g + 1))
        if g > 0:
            first.append(functools.partial(return_across, g - 1))
            last.append(functools.partial(return_column, g - 1))
        fill_pool(g, n, n_far, tab, own_kv, banks[g][0], pool_ref)
        cuts = sorted({0, min(1, chunks), chunks // 2, chunks})
        for i in range(len(cuts) - 1):
            attend(
                g, per_group, chunk_tokens, cuts[i], cuts[i + 1],
                picked_ref, q_ref, do_ref, dq_ref, pool_ref, banks[g][1],
            )
            for step in (first if i == 0 else last if i == len(cuts) - 2 else []):
                step()
        if g + 1 < groups:
            gather_end(g + 1)
        return_start(g)
    final = groups - 1
    return_across(final)
    return_column(final)
    for g in range(groups):
        return_end(g)
    for g in range(groups):
        gather_drain(g)
        return_drain(g)
    key_out[...] = mix_ref[0, : own_rows * groups].astype(jnp.bfloat16)
    value_out[...] = mix_ref[1, : own_rows * groups].astype(jnp.bfloat16)


def columns_of(mesh, n):
    spots = [getattr(d, "coords", None) for d in mesh.devices.reshape(-1, n)[0]]
    if None in spots or n % 2:
        return 1
    cols = sum(spot[2] == spots[0][2] for spot in spots) // 2
    return 2 if cols == 2 and n % 4 == 0 else 1


def local(cols, queries, keys, values, grad_out, selected):
    tokens, head_count, dh = queries.shape
    groups = keys.shape[1]
    own_blocks = tokens // BLK
    n = lax.axis_size("ctx")
    depth = n // (2 * cols)
    fetched = min(n - 2, max(selected.shape[2] - own_blocks, 4)) + 1
    slots = -(-(own_blocks + fetched) // 16) * 16
    far_rows = -(-fetched // 8) * 8
    pool_rows = (own_blocks + fetched) * BLK
    chosen = selected.transpose(1, 2, 0)
    own_kv = jnp.stack([keys, values], axis=0).transpose(2, 0, 1, 3)
    piece = (2, own_blocks, BLK, dh)
    own_kv = own_kv.reshape((groups,) + piece)
    vmem = pl.BlockSpec(memory_space=pltpu.VMEM)
    any_spec = pl.BlockSpec(memory_space=pl.ANY)
    bank = [
        pltpu.VMEM((n,) + piece, jnp.bfloat16),
        pltpu.VMEM((2, pool_rows // BLK, BLK, dh), jnp.float32),
        pltpu.VMEM((n // 2, ID_ROWS + 2 * BLK, dh), jnp.bfloat16),
        pltpu.VMEM((n // 2, ID_ROWS + 2 * BLK, dh), jnp.bfloat16),
        pltpu.VMEM((depth,) + piece, jnp.bfloat16),
        pltpu.VMEM((depth,) + piece, jnp.bfloat16),
        pltpu.VMEM((depth,) + piece, jnp.bfloat16),
        pltpu.VMEM((depth,) + piece, jnp.bfloat16),
        pltpu.VMEM(piece, jnp.float32),
    ]
    dma = pltpu.SemaphoreType.DMA
    dq, key_grad, value_grad = pl.pallas_call(
        functools.partial(fused_kernel, n, cols, fetched, min(tokens, 32), groups),
        out_shape=(
            jax.ShapeDtypeStruct(queries.shape, jnp.bfloat16),
            jax.ShapeDtypeStruct((tokens * groups, dh), jnp.bfloat16),
            jax.ShapeDtypeStruct((tokens * groups, dh), jnp.bfloat16),
        ),
        in_specs=[vmem, any_spec, any_spec, vmem],
        out_specs=(vmem, vmem, vmem),
        scratch_shapes=bank * groups + [
            pltpu.VMEM((groups, slots, tokens), jnp.bfloat16),
            pltpu.VMEM((groups, n + far_rows, LANES), jnp.int32),
            pltpu.SMEM((groups, n + far_rows, LANES), jnp.int32),
            pltpu.VMEM(queries.shape, jnp.bfloat16),
            pltpu.VMEM(queries.shape, jnp.bfloat16),
            pltpu.VMEM((2, tokens * groups + 8, dh), jnp.float32),
            dma((3,)),
            pltpu.VMEM((2, pool_rows, dh), jnp.bfloat16),
            pltpu.VMEM((depth,) + piece, jnp.float32),
            dma((groups, depth)),
            dma((groups, depth)),
            dma((groups, n)),
            dma((groups, n)),
            dma((groups, 2)),
            dma((groups, depth)),
            dma((groups, depth)),
            dma((groups, depth)),
            dma((groups, depth)),
        ],
        compiler_params=pltpu.CompilerParams(collective_id=0, has_side_effects=True),
    )(chosen, queries, grad_out, own_kv)
    return dq, key_grad.reshape(keys.shape), value_grad.reshape(values.shape)


def solution(mesh):
    spec = P(("rep", "ctx"), None, None)
    cols = columns_of(mesh, mesh.shape["ctx"])
    return jax.shard_map(
        functools.partial(local, cols),
        mesh=mesh,
        in_specs=(spec,) * 5,
        out_specs=(spec,) * 3,
        check_vma=False,
    )
```

profile of v0, /device:TPU:0, one launch (start us, length us, event | category | flops | bytes accessed | tf_op | source)
XLA Modules:
  0.0 58.2 jit_solution(17522408615323757775)
XLA Ops:
  0.6 1.1 %maximum_bitcast_fusion = bf16[2,2,128,128]{3,0,2,1:T(2,128)(2,1)S(1)} fusion(bf16[1,128,2,128]{3,2,1,0:T(2,128)(2,1)} %bitcast.11, bf16[1,128,2,128]{3,2,1,0:T(2,128)(2,1)} %bitcast.12), kind=kLoop, calls=%fused_computation | loop fusion | flops 65536 | bytes 262144 | tf_op jit(solution)/shard_map/transpose | solution.py:438
  1.7 0.7 %copy.8 = bf16[2,2,128,128]{3,2,1,0:T(8,128)(2,1)} copy(bf16[2,2,128,128]{3,0,2,1:T(2,128)(2,1)S(1)} %maximum_bitcast_fusion) | data formatting | bytes 262144 | tf_op jit(solution)/shard_map/transpose | solution.py:438
  2.4 52.0 %shard_map.76 = (bf16[128,32,128]{2,1,0:T(8,128)(2,1)}, bf16[256,128]{1,0:T(8,128)(2,1)}, bf16[256,128]{1,0:T(8,128)(2,1)}) custom-call(s32[2,8,128]{2,1,0:T(8,128)} %bitcast.13, bf16[128,32,128]{2,1,0:T(8,128)(2,1)} %q_hbm.1, bf16[128,32,128]{2,1,0:T(8,128)(2,1)} %do_hbm.1, bf16[2,2,2,64,128]{4,3,2,1,0:T(8,128)(2,1)} %bitcast.8), custom_call_target="tpu_custom_call" | custom-call | tf_op jit(solution)/shard_map/pallas_call | solution.py:455
  54.4 0.0 copy-start.1
  54.4 2.3 %copy.12 = bf16[128,32,128]{2,1,0:T(8,128)(2,1)} copy(bf16[128,32,128]{2,1,0:T(8,128)(2,1)} %get-tuple-element.12) | data formatting | bytes 2097152
  56.7 0.0 copy-done.1
  56.7 0.0 copy-start
  56.7 0.6 %copy.13 = bf16[128,2,128]{2,1,0:T(2,128)(2,1)} copy(bf16[128,2,128]{2,1,0:T(2,128)(2,1)S(1)} %bitcast.10) | data formatting | bytes 131072
  57.3 0.2 copy-done
  57.6 0.6 %copy.14 = bf16[128,2,128]{2,1,0:T(2,128)(2,1)} copy(bf16[128,2,128]{2,1,0:T(2,128)(2,1)S(1)} %bitcast.9) | data formatting | bytes 131072
Async XLA Ops:
  54.4 2.3 %copy-start.1 = (bf16[256,128]{1,0:T(8,128)(2,1)S(1)}, bf16[256,128]{1,0:T(8,128)(2,1)}, u32[]{:S(2)}) copy-start(bf16[256,128]{1,0:T(8,128)(2,1)} %get-tuple-element.7) | copy-start | bytes 196612
  56.7 0.9 %copy-start = (bf16[256,128]{1,0:T(8,128)(2,1)S(1)}, bf16[256,128]{1,0:T(8,128)(2,1)}, u32[]{:S(2)}) copy-start(bf16[256,128]{1,0:T(8,128)(2,1)} %get-tuple-element.8) | copy-start | bytes 196612
where the time goes:
time: 58.4 us; the launch traced here: 58.2 us
  Pallas kernels  52 us (89%)
  local copies, waits for them, and re-layouts  4.46 us (8%)
  other arithmetic  1.06 us (2%)
  between operations  0.65 us (1%)
    pallas_call x1, Pallas kernels, local(): pl.pallas_call(functools.partial(fused_kernel, n, cols, fetched, min(toke...  52 us
    unnamed x7, local copies, waits for them, and re-layouts  3.79 us

commit v1 on v0

--- a/solution.py
+++ b/solution.py
@@ -136,13 +136,13 @@
 
 def fused_kernel(
     n, cols, n_far, chunk_tokens, groups,
-    sel_ref, q_hbm, do_hbm, own_kv, dq_ref, key_out, value_out, *scratch,
+    sel_ref, q_hbm, do_hbm, k_in, v_in, dq_ref, key_out, value_out, *scratch,
 ):
     per_bank = 9
     banks = [scratch[g * per_bank : (g + 1) * per_bank] for g in range(groups)]
     (
         picked_ref, tab_ref, tab, q_ref, do_ref, mix_ref, in_sem, pool_ref, mid_ref, col_send, y_send, sib_send, recv_sem,
-        rs_sem, ry_send, ry_recv, rz_send, rz_recv,
+        rs_sem, ry_send, ry_recv, rz_send, rz_recv, own_kv,
     ) = scratch[groups * per_bank :]
     depth = n // (2 * cols)
     chips = n // 2
@@ -164,6 +164,12 @@
     def device(zz, yy, cc):
         return 2 * (zz * cols + yy) + cc
 
+    def near(k):
+        room = jnp.minimum(z, depth - 1 - z)
+        step = jnp.where(lax.rem(k, 2) == 1, -((k + 1) // 2), k // 2)
+        side = jnp.where(z < depth - 1 - z, k - room, room - k)
+        return z + jnp.where(k <= 2 * room, step, side)
+
     def remote(src, dst, send, recv, peer):
         return pltpu.make_async_remote_copy(
             src_ref=src,
@@ -175,7 +181,7 @@
         )
 
     def col_copy(g, k):
-        peer = device(lax.rem(z + k, depth), y, core)
+        peer = device(near(k), y, core)
         return remote(
             own_kv.at[g], banks[g][0].at[me], col_send.at[g, k], recv_sem.at[g, me], peer
         )
@@ -203,7 +209,7 @@
     def gather_column(g):
         @pl.loop(1, depth)
         def _(k):
-            from_z = lax.rem(z + depth - k, depth)
+            from_z = near(k)
             src = device(from_z, y, core)
             await_piece(g, src)
             if cols > 1:
@@ -214,7 +220,7 @@
         if cols > 1:
             @pl.loop(0, depth)
             def _(k):
-                src = device(lax.rem(z + depth - k, depth), other_y, core)
+                src = device(jnp.where(k == 0, z, near(k)), other_y, core)
                 await_piece(g, src)
                 pass_on(g, src, sib_send.at[g, src], sib).start()
 
@@ -369,6 +375,11 @@
     ]
     for load in loads:
         load.start()
+    for kv, source in enumerate((k_in, v_in)):
+        mix_ref[kv, : own_rows * groups] = source[...].astype(jnp.float32)
+        for g in range(groups):
+            rows = mix_ref[kv, pl.ds(g, own_rows, stride=groups), :].astype(jnp.bfloat16)
+            own_kv[g, kv] = rows.reshape(own_blocks, BLK, dh)
     pl.semaphore_wait(barrier, depth + cols - 1)
     for g in range(groups):
         gather_start(g)
@@ -416,6 +427,28 @@
     value_out[...] = mix_ref[1, : own_rows * groups].astype(jnp.bfloat16)
 
 
+def store_kernel(*refs):
+    count = (len(refs) - 1) // 2
+    sem = refs[-1]
+    copies = [
+        pltpu.make_async_copy(refs[i], refs[count + i], sem.at[i]) for i in range(count)
+    ]
+    for copy in copies:
+        copy.start()
+    for copy in copies:
+        copy.wait()
+
+
+def store(arrays):
+    return pl.pallas_call(
+        store_kernel,
+        out_shape=tuple(jax.ShapeDtypeStruct(a.shape, a.dtype) for a in arrays),
+        in_specs=[pl.BlockSpec(memory_space=pltpu.VMEM)] * len(arrays),
+        out_specs=(pl.BlockSpec(memory_space=pl.ANY),) * len(arrays),
+        scratch_shapes=[pltpu.SemaphoreType.DMA((len(arrays),))],
+    )(*arrays)
+
+
 def columns_of(mesh, n):
     spots = [getattr(d, "coords", None) for d in mesh.devices.reshape(-1, n)[0]]
     if None in spots or n % 2:
@@ -435,9 +468,7 @@
     far_rows = -(-fetched // 8) * 8
     pool_rows = (own_blocks + fetched) * BLK
     chosen = selected.transpose(1, 2, 0)
-    own_kv = jnp.stack([keys, values], axis=0).transpose(2, 0, 1, 3)
     piece = (2, own_blocks, BLK, dh)
-    own_kv = own_kv.reshape((groups,) + piece)
     vmem = pl.BlockSpec(memory_space=pltpu.VMEM)
     any_spec = pl.BlockSpec(memory_space=pl.ANY)
     bank = [
@@ -455,11 +486,11 @@
     dq, key_grad, value_grad = pl.pallas_call(
         functools.partial(fused_kernel, n, cols, fetched, min(tokens, 32), groups),
         out_shape=(
-            jax.ShapeDtypeStruct(queries.shape, jnp.bfloat16),
-            jax.ShapeDtypeStruct((tokens * groups, dh), jnp.bfloat16),
-            jax.ShapeDtypeStruct((tokens * groups, dh), jnp.bfloat16),
+            pltpu.VMEM(queries.shape, jnp.bfloat16),
+            pltpu.VMEM((tokens * groups, dh), jnp.bfloat16),
+            pltpu.VMEM((tokens * groups, dh), jnp.bfloat16),
         ),
-        in_specs=[vmem, any_spec, any_spec, vmem],
+        in_specs=[vmem, any_spec, any_spec, vmem, vmem],
         out_specs=(vmem, vmem, vmem),
         scratch_shapes=bank * groups + [
             pltpu.VMEM((groups, slots, tokens), jnp.bfloat16),
@@ -480,9 +511,19 @@
             dma((groups, depth)),
             dma((groups, depth)),
             dma((groups, depth)),
+            pltpu.VMEM((groups,) + piece, jnp.bfloat16),
         ],
         compiler_params=pltpu.CompilerParams(collective_id=0, has_side_effects=True),
-    )(chosen, queries, grad_out, own_kv)
+    )(
+        chosen,
+        queries,
+        grad_out,
+        keys.reshape(tokens * groups, dh),
+        values.reshape(tokens * groups, dh),
+    )
+    held = (dq, key_grad, value_grad)
+    held = [pltpu.with_memory_space_constraint(a, pltpu.VMEM) for a in held]
+    dq, key_grad, value_grad = store(held)
     return dq, key_grad.reshape(keys.shape), value_grad.reshape(values.shape)
 
 

time: 58.4 us -> 51.4 us (0.88)
  local copies, waits for them, and re-layouts: 4.46 us -> 0 us
  Pallas kernels: 52 us -> 50.6 us
  other arithmetic: 1.06 us -> 0 us
    unnamed x7 -> x0, local copies, waits for them, and re-layouts: 3.79 us -> none
    pallas_call x1, Pallas kernels: 52 us -> 49.6 us  [local(): pl.pallas_call(functools.partial(fused_kernel, n, cols, fetched, min(toke...]
    transpose x1 -> x0, other arithmetic: 1.06 us -> none  [local(): own_kv = jnp.stack([keys, values], axis=0).transpose(2, 0, 1, 3)]
    pallas_call x0 -> x1, Pallas kernels: none -> 1.02 us  [store(): pl.pallas_call(store_kernel, out_shape=tuple((jax.ShapeDtypeStruct(a.shap...]
    transpose x1 -> x0, local copies, waits for them, and re-layouts: 0.67 us -> none  [local(): own_kv = jnp.stack([keys, values], axis=0).transpose(2, 0, 1, 3)]
where the time goes in v1:
time: 51.4 us; the launch traced here: 51.3 us
  Pallas kernels  50.6 us (98%)
  between operations  0.64 us (1%)
    pallas_call x1, Pallas kernels, local(): pl.pallas_call(functools.partial(fused_kernel, n, cols, fetched, min(toke...  49.6 us

profile of v1, /device:TPU:0, one launch (start us, length us, event | category | flops | bytes accessed | tf_op | source)
XLA Modules:
  0.0 51.3 jit_solution(16369124507511270751)
XLA Ops:
  0.6 49.6 %shard_map.76 = (bf16[128,32,128]{2,1,0:T(8,128)(2,1)S(1)}, bf16[256,128]{1,0:T(8,128)(2,1)S(1)}, bf16[256,128]{1,0:T(8,128)(2,1)S(1)}) custom-call(s32[2,8,128]{2,1,0:T(8,128)} %bitcast.7, bf16[128,32,128]{2,1,0:T(8,128)(2,1)} %q_hbm.1, bf16[128,32,128]{2,1,0:T(8,128)(2,1)} %do_hbm.1, bf16[256,128]{1,0:T(8,128)(2,1)} %bitcast.5, bf16[256,128]{1,0:T(8,128)(2,1)} %bitcast.6), custom_call_target="tpu_custom_call" | custom-call | tf_op jit(solution)/shard_map/pallas_call | solution.py:486
  50.2 1.0 %shard_map.77 = (bf16[128,32,128]{2,1,0:T(8,128)(2,1)}, bf16[256,128]{1,0:T(8,128)(2,1)}, bf16[256,128]{1,0:T(8,128)(2,1)}) custom-call(bf16[128,32,128]{2,1,0:T(8,128)(2,1)S(1)} %get-tuple-element.9.refs_0_, bf16[256,128]{1,0:T(8,128)(2,1)S(1)} %get-tuple-element.10.refs_1_, bf16[256,128]{1,0:T(8,128)(2,1)S(1)} %get-tuple-element.11.refs_2_), custom_call_target="tpu_custom_call" | custom-call | tf_op jit(solution)/shard_map/pallas_call | solution.py:443

commit v2 on v1

v2 whole, which is shorter than its diff:
```python
import functools
import math

import jax
import jax.numpy as jnp
from jax import lax
from jax.experimental import pallas as pl
from jax.experimental.pallas import tpu as pltpu
from jax.sharding import PartitionSpec as P

BLK = 64
NEG = -1e30
BAND = 3
LANES = 128
LOG2E = math.log2(math.e)
NT = (((1,), (1,)), ((), ()))
NN = (((1,), (0,)), ((), ()))


def rows_of(ref, c, chunk_tokens, heads):
    part = ref[c * chunk_tokens : (c + 1) * chunk_tokens, heads, :]
    return part.reshape(part.shape[0] * part.shape[1], part.shape[2])


def bands(total):
    step = BLK * BAND
    return [(lo, min(lo + step, total)) for lo in range(0, total, step)]


def fold(x, op):
    return op(x.reshape(x.shape[0] // 8, 8, x.shape[1]), axis=0)


def fill_bias(picked, per_group, chunk_tokens, bias_ref, own_bias_ref):
    tokens = picked.shape[1]
    rows = chunk_tokens * per_group
    shift = per_group.bit_length() - 1

    @pl.loop(0, tokens // chunk_tokens)
    def _(c):
        row_tok = c * chunk_tokens + (lax.broadcasted_iota(jnp.int32, (tokens, rows), 1) >> shift)
        tok = lax.broadcasted_iota(jnp.int32, (tokens, rows), 0)
        spread = jnp.where(row_tok == tok, 1.0, 0.0).astype(jnp.bfloat16)
        seen = lax.dot_general(picked, spread, NN, preferred_element_type=jnp.float32)
        bias = (seen - 1.0) * (-NEG)
        bias_ref[c] = bias
        for j in range(tokens // BLK):
            at = slice(j * BLK, (j + 1) * BLK)
            own_bias_ref[c, at] = jnp.where(tok[at] <= row_tok[at], bias[j : j + 1], NEG)


class Weigh:
    def __init__(self, heads, chunk_tokens, bias, own_bias, q_ref, do_ref, keys, s_ref, e_ref, acc_ref):
        self.__dict__.update(locals())
        self.peak, self.inv = {}, {}

    def scores(self, c):
        tokens, _, dh = self.q_ref.shape
        q = rows_of(self.q_ref, c, self.chunk_tokens, self.heads)
        peak = None
        for lo, hi in bands(self.keys.shape[0]):
            s = lax.dot_general(self.keys[lo:hi], q, NT, preferred_element_type=jnp.float32)
            for j in range(lo // BLK, hi // BLK):
                part = s[j * BLK - lo : (j + 1) * BLK - lo]
                if j < tokens // BLK:
                    part = part + self.own_bias[c, j * BLK : (j + 1) * BLK]
                else:
                    part = part + self.bias[c, j : j + 1]
                self.s_ref[c % 2, j * BLK : (j + 1) * BLK] = part
                top = fold(part, jnp.max)
                peak = top if peak is None else jnp.maximum(peak, top)
            yield
        log_scale = LOG2E / math.sqrt(dh)
        self.peak[c] = jnp.max(peak, axis=0, keepdims=True) * log_scale

    def exponents(self, c):
        dh = self.q_ref.shape[2]
        log_scale = LOG2E / math.sqrt(dh)
        total = None
        for lo, hi in bands(self.keys.shape[0]):
            for j in range(lo // BLK, hi // BLK):
                at = slice(j * BLK, (j + 1) * BLK)
                e = jnp.exp2(self.s_ref[c % 2, at] * log_scale - self.peak[c])
                self.e_ref[c, at] = e
                part = fold(e, jnp.sum)
                total = part if total is None else total + part
            yield
        self.inv[c] = 1.0 / jnp.sum(total, axis=0, keepdims=True)

    def products(self, c):
        do = rows_of(self.do_ref, c, self.chunk_tokens, self.heads)
        for lo, hi in bands(self.keys.shape[0]):
            p = self.e_ref[c, lo:hi] * self.inv[c]
            self.e_ref[c, lo:hi] = p
            dv = lax.dot_general(p.astype(jnp.bfloat16), do, NN, preferred_element_type=jnp.float32)
            dv = dv.reshape((hi - lo) // BLK, BLK, dv.shape[1])
            at = slice(lo // BLK, hi // BLK)
            self.acc_ref[at] = dv if c == 0 else self.acc_ref[at] + dv
            yield


class Slope:
    def __init__(self, heads, chunk_tokens, q_ref, do_ref, values, s_ref, e_ref, ds_ref, acc_ref):
        self.__dict__.update(locals())
        self.inner = {}

    def scores(self, c):
        do = rows_of(self.do_ref, c, self.chunk_tokens, self.heads)
        total = None
        for lo, hi in bands(self.values.shape[0]):
            dp = lax.dot_general(self.values[lo:hi], do, NT, preferred_element_type=jnp.float32)
            for j in range(lo // BLK, hi // BLK):
                part = dp[j * BLK - lo : (j + 1) * BLK - lo]
                self.s_ref[c % 2, j * BLK : (j + 1) * BLK] = part
                part = fold(part * self.e_ref[c, j * BLK : (j + 1) * BLK], jnp.sum)
                total = part if total is None else total + part
            yield
        self.inner[c] = jnp.sum(total, axis=0, keepdims=True)

    def products(self, c):
        q = rows_of(self.q_ref, c, self.chunk_tokens, self.heads)
        for lo, hi in bands(self.values.shape[0]):
            dp = self.s_ref[c % 2, lo:hi]
            ds = (self.e_ref[c, lo:hi] * (dp - self.inner[c])).astype(jnp.bfloat16)
            self.ds_ref[c, lo:hi] = ds
            dk = lax.dot_general(ds, q, NN, preferred_element_type=jnp.float32)
            dk = dk.reshape((hi - lo) // BLK, BLK, dk.shape[1])
            at = slice(lo // BLK, hi // BLK)
            self.acc_ref[at] = dk if c == 0 else self.acc_ref[at] + dk
            yield


def side_by_side(parts):
    parts = list(parts)
    while parts:
        parts = [part for part in parts if next(part, parts) is None]


def pipelined(phases, chunks, between):
    depth = len(phases)
    for t in range(chunks + depth - 1):
        live = [(i, t - i) for i in range(depth) if 0 <= t - i < chunks]
        side_by_side(phases[i](c) for i, c in reversed(live))
        between(t)


def query_grad(c, heads, chunk_tokens, keys_t, ds_ref, dq_ref):
    dh = keys_t.shape[0]
    t0 = pl.multiple_of(c * chunk_tokens, chunk_tokens)
    dqt = lax.dot_general(keys_t, ds_ref[c], NN, preferred_element_type=jnp.float32)
    dq = (dqt * (1.0 / math.sqrt(dh))).T.astype(jnp.bfloat16)
    per_group = heads.stop - heads.start
    dq_ref[pl.ds(t0, chunk_tokens), heads, :] = dq.reshape(chunk_tokens, per_group, dh)


def fill_tables(g, n, me, n_far, own_blocks, sel_ref, picked_ref, tab_ref):
    sel = sel_ref[g]
    tokens = sel.shape[1]
    shift = own_blocks.bit_length() - 1
    owner = sel >> shift
    block = sel & (own_blocks - 1)
    peers = lax.broadcasted_iota(jnp.int32, (n, tokens), 0)
    code = jnp.zeros((n, tokens), jnp.float32)
    for i in range(sel.shape[0]):
        mark = (block[i : i + 1] + 1).astype(jnp.float32)
        code = jnp.maximum(code, jnp.where(owner[i : i + 1] == peers, mark, 0.0))
    code = jnp.broadcast_to(jnp.max(code, axis=1, keepdims=True), (n, LANES))
    peers = lax.broadcasted_iota(jnp.int32, (n, LANES), 0)
    code = jnp.where(peers == me, 0.0, code)
    live = jnp.where(code > 0.0, 1.0, 0.0)
    before = lax.broadcasted_iota(jnp.int32, (n, n), 1) < lax.broadcasted_iota(jnp.int32, (n, n), 0)
    before = jnp.where(before, 1.0, 0.0).astype(jnp.bfloat16)
    slot = lax.dot_general(before, live.astype(jnp.bfloat16), NN, preferred_element_type=jnp.float32)
    far = jnp.maximum(code - 1.0, 0.0)
    lane = lax.broadcasted_iota(jnp.int32, (n, LANES), 1)
    kept = jnp.minimum(slot, float(n_far - 1))
    entry = jnp.where(lane == 0, kept, jnp.where(lane == 1, live, far))
    tab_ref[g, :n, :] = entry.astype(jnp.int32)
    peer = peers.astype(jnp.float32)
    now = me * own_blocks + (lax.broadcasted_iota(jnp.int32, (1, tokens), 1) >> BLK.bit_length() - 1)
    slots = picked_ref.shape[1]
    row = lax.broadcasted_iota(jnp.int32, (slots, tokens), 0)
    far_rows = tab_ref.shape[1] - n
    far_row = lax.broadcasted_iota(jnp.int32, (far_rows, LANES), 0)
    far_lane = lax.broadcasted_iota(jnp.int32, (far_rows, LANES), 1)
    far_entry = jnp.zeros((far_rows, LANES), jnp.float32)
    picked = jnp.zeros((slots, tokens), jnp.float32)
    for i in range(own_blocks + n_far):
        if i < own_blocks:
            ids = jnp.full((1, tokens), me * own_blocks + i, jnp.int32)
        else:
            hit = (live > 0.0) & (slot == float(i - own_blocks))
            who = jnp.max(jnp.where(hit, peer, -1.0), axis=0, keepdims=True)
            which = jnp.max(jnp.where(hit, far, 0.0), axis=0, keepdims=True)
            ids = jnp.max(who * own_blocks + which, axis=1, keepdims=True).astype(jnp.int32)
            ids = jnp.broadcast_to(ids, (1, tokens))
            here = jnp.where(far_lane == 0, jnp.maximum(who, 0.0), which)
            far_entry = jnp.where(far_row == i - own_blocks, here, far_entry)
        seen = jnp.max(jnp.where(sel == ids, 1.0, 0.0), axis=0, keepdims=True)
        seen = jnp.where(ids <= now, seen, 0.0)
        picked = jnp.where(row == i, seen, picked)
    tab_ref[g, n:, :] = far_entry.astype(jnp.int32)
    picked_ref[g] = picked.astype(jnp.bfloat16)


def fused_kernel(
    n, cols, n_far, chunk_tokens, groups,
    sel_hbm, q_hbm, do_hbm, k_hbm, v_hbm, dq_ref, key_out, value_out,
    sel_ref, q_ref, do_ref, raw_ref, mix_ref, own, pool, acc, s_ref, e_ref, bias_ref, own_bias_ref, ds_ref,
    picked_ref, tab_ref, mate_tab_ref, tab, box, box_in, z_box, z_in, total_ref,
    in_sem, tab_sem, zs, zr, ys, yr, ss, sr, box_send, box_recv, rz_send, rz_recv, *banks,
):
    gaths, mate_tabs = list(banks[: 2 * groups]), list(banks[2 * groups :])
    depth = n // (2 * cols)
    chips = n // 2
    me = lax.axis_index("ctx")
    core = lax.rem(me, 2)
    chip = me // 2
    y = lax.rem(chip, cols)
    z = chip // cols
    sib = 2 * chip + 1 - core
    other_y = cols - 1 - y
    y_peer = 2 * (z * cols + other_y) + core
    own_blocks = own.shape[1]
    own_rows = own_blocks * BLK
    dh = own.shape[3]
    per_group = q_ref.shape[1] // groups
    chunks = q_ref.shape[0] // chunk_tokens
    scaling = 1.0 / math.sqrt(dh)
    pieces = 2 * groups
    near_max = depth - 1

    def device(zz, yy, cc):
        return 2 * (zz * cols + yy) + cc

    def near(k):
        room = jnp.minimum(z, depth - 1 - z)
        step = jnp.where(lax.rem(k, 2) == 1, -((k + 1) // 2), k // 2)
        side = jnp.where(z < depth - 1 - z, k - room, room - k)
        return z + jnp.where(k <= 2 * room, step, side)

    def remote(src, dst, send, recv, peer):
        return pltpu.make_async_remote_copy(
            src_ref=src,
            dst_ref=dst,
            send_sem=send,
            recv_sem=recv,
            device_id={"ctx": peer},
            device_id_type=pl.DeviceIdType.MESH,
        )

    def direct(p):
        return p < 2

    def z_send(p, src, from_z, to_z):
        dst = gaths[p].at[core, from_z * cols + y]
        return remote(src, dst, zs.at[p], zr.at[p, from_z], device(to_z, y, core))

    def z_wait(p, from_z):
        spot = gaths[p].at[core, from_z * cols + y]
        remote(spot, spot, zs.at[p], zr.at[p, from_z], y_peer if cols > 1 else sib).wait_recv()

    def y_send(p, src, from_z):
        dst = gaths[p].at[core, from_z * cols + y]
        return remote(src, dst, ys.at[p], yr.at[p, from_z], y_peer)

    def y_wait(p, from_z):
        spot = gaths[p].at[core, from_z * cols + other_y]
        remote(spot, spot, ys.at[p], yr.at[p, from_z], y_peer).wait_recv()

    def sib_send(p, src, q):
        return remote(src, gaths[p].at[core, q], ss.at[p], sr.at[p], sib)

    def gather_start(p):
        if cols > 1:
            y_send(p, own.at[p], z).start()

        if direct(p):
            @pl.loop(1, depth)
            def _(k):
                z_send(p, own.at[p], z, near(depth - k)).start()
        else:
            for to_z in (z - 1, z + 1):
                @pl.when((to_z >= 0) & (to_z < depth))
                def _():
                    z_send(p, own.at[p], z, to_z).start()

        sib_send(p, own.at[p], chip).start()

    def span(i):
        return 1 + i * near_max // 3, 1 + (i + 1) * near_max // 3

    def each_at(d, visit):
        for side in (-1, 1):
            from_z = z + side * d

            @pl.when((from_z >= 0) & (from_z < depth))
            def _():
                visit(from_z, z - side)

    def z_step(p, i):
        lo, hi = span(i)

        def visit(from_z, to_z):
            q = from_z * cols + y
            spot = gaths[p].at[core, q]
            z_wait(p, from_z)
            if not direct(p):
                @pl.when((to_z >= 0) & (to_z < depth))
                def _():
                    z_send(p, spot, from_z, to_z).start()


            if cols > 1:
                y_send(p, spot, from_z).start()
            sib_send(p, spot, q).start()

        @pl.loop(lo, hi)
        def _(d):
            each_at(d, visit)

    def y_step(p, i):
        if cols == 1:
            return

        def visit(from_z, to_z):
            q = from_z * cols + other_y
            y_wait(p, from_z)
            sib_send(p, gaths[p].at[core, q], q).start()

        if i == 0:
            visit(z, z)
        else:
            lo, hi = span(i - 1)

            @pl.loop(lo, hi)
            def _(d):
                each_at(d, visit)

    def gather_end(p):
        spot = gaths[p].at[1 - core]
        remote(spot, spot, ss.at[p], sr.at[p], sib).wait_recv()

    def z_drain(p, count):
        @pl.loop(0, count)
        def _(k):
            z_send(p, own.at[p], z, z).wait_send()

    def gather_drain(p):
        spot = gaths[p].at[core]
        remote(spot, spot, ss.at[p], sr.at[p], sib).wait_send()
        if direct(p):
            z_drain(p, depth - 1)
        else:
            for more, count in ((z > 0, depth - z), (z < depth - 1, z + 1)):
                @pl.when(more)
                def _():
                    z_drain(p, count)

        if cols > 1:
            part = gaths[p].at[core, pl.ds(0, depth)]
            remote(part, part, ys.at[p], yr.at[p, z], y_peer).wait_send()

    def fill_pool(p):
        g = p // 2
        pool[p, :own_rows, :] = own[p].reshape(own_rows, dh)
        for s in range(n_far):
            owner = jnp.clip(tab[g, n + s, 0], 0, n - 1)
            block = jnp.clip(tab[g, n + s, 1], 0, own_blocks - 1)
            lo = own_rows + s * BLK
            pool[p, lo : lo + BLK, :] = gaths[p][owner & 1, owner >> 1, block]

    mates = [(y, 1 - core)] + ([(other_y, core), (other_y, 1 - core)] if cols > 1 else [])

    def mate_copy(p, m, zz):
        return remote(
            box.at[p, m, zz], box_in.at[p, m, zz], box_send.at[p, m], box_recv.at[p, m, zz],
            device(z, *mates[m]),
        )

    def z_copy(p, to_z):
        return remote(
            z_box.at[p, to_z], z_in.at[p, z], rz_send.at[p], rz_recv.at[p], device(to_z, y, core)
        )

    def factor(p):
        return scaling if p % 2 == 0 else 1.0

    def far_part(p, dest):
        return acc[p, own_blocks + jnp.clip(tab[p // 2, dest, 0], 0, n_far - 1)]

    def far_first(k):
        return jnp.where(k == depth, z, near(jnp.maximum(depth - k, 1)))

    def return_start(p):
        g = p // 2

        @pl.loop(1, depth + 1)
        def _(k):
            zz = far_first(k)
            for m, (yy, cc) in enumerate(mates):
                dest = device(zz, yy, cc)
                keep = tab[g, dest, 1].astype(jnp.float32) * factor(p)
                box[p, m, zz] = (far_part(p, dest) * keep).astype(jnp.bfloat16)
            for m in range(len(mates)):
                mate_copy(p, m, zz).start()

    def merged(p, zz):
        g = p // 2
        dest = device(zz, y, core)
        for m in range(len(mates)):
            mate_copy(p, m, zz).wait_recv()
        parts = [far_part(p, dest) * (tab[g, dest, 1].astype(jnp.float32) * factor(p))]
        tables = [tab] + mate_tabs
        for m in range(len(mates)):
            parts.append(box_in[p, m, zz].astype(jnp.float32))
        for b in range(own_blocks):
            total = None
            for table, part in zip(tables, parts):
                share = part * jnp.where(table[g, dest, 2] == b, 1.0, 0.0)
                total = share if total is None else total + share
            yield b, total

    def return_column(p, i):
        lo, hi = span(i)

        @pl.loop(lo, hi)
        def _(k):
            to_z = far_first(k)
            for b, part in merged(p, to_z):
                z_box[p, to_z, b] = part.astype(jnp.bfloat16)
            z_copy(p, to_z).start()

    def return_own(p):
        for b, part in merged(p, z):
            total_ref[p, b] = part + acc[p, b] * factor(p)

    def return_end(p):
        part = z_in.at[p, pl.ds(0, depth - 1)]
        remote(part, part, rz_send.at[p], rz_recv.at[p], sib).wait_recv()

        @pl.loop(1, depth)
        def _(k):
            from_z = near(k)
            total_ref[p] += z_in[p, from_z].astype(jnp.float32)

        whole = total_ref[p].reshape(own_rows, dh)
        mix_ref[p % 2, pl.ds(p // 2, own_rows, stride=groups), :] = whole

    def return_drain(p):
        for m in range(len(mates)):
            part = box.at[p, m]
            remote(part, part, box_send.at[p, m], box_recv.at[p, m, 0], sib).wait_send()
        part = z_box.at[p, pl.ds(0, depth - 1)]
        remote(part, part, rz_send.at[p], rz_recv.at[p], sib).wait_send()

    barrier = pltpu.get_barrier_semaphore()

    def greet(peer):
        pl.semaphore_signal(
            barrier, inc=1, device_id={"ctx": peer}, device_id_type=pl.DeviceIdType.MESH
        )

    @pl.loop(1, depth)
    def _(k):
        greet(device(near(k), y, core))

    for yy, cc in mates:
        greet(device(z, yy, cc))
    loads = [
        pltpu.make_async_copy(src, dst, in_sem.at[i])
        for i, (src, dst) in enumerate([
            (k_hbm, raw_ref.at[0]), (v_hbm, raw_ref.at[1]), (sel_hbm, sel_ref), (q_hbm, q_ref), (do_hbm, do_ref),
        ])
    ]
    for load in loads:
        load.start()
    for kv in range(2):
        loads[kv].wait()
        mix_ref[kv, : own_rows * groups] = raw_ref[kv].astype(jnp.float32)
        for g in range(groups):
            rows = mix_ref[kv, pl.ds(g, own_rows, stride=groups), :].astype(jnp.bfloat16)
            own[2 * g + kv] = rows.reshape(own_blocks, BLK, dh)
    pl.semaphore_wait(barrier, depth - 1 + len(mates))
    for p in range(pieces):
        gather_start(p)
    loads[2].wait()
    for g in range(groups):
        fill_tables(g, n, me, n_far, own_blocks, sel_ref, picked_ref, tab_ref)
    to_scalars = pltpu.make_async_copy(tab_ref, tab, in_sem.at[5])
    to_scalars.start()
    to_mates = [
        remote(
            tab_ref, mate_tab_ref.at[m], tab_sem.at[0, m], tab_sem.at[1, m], device(z, yy, cc)
        )
        for m, (yy, cc) in enumerate(mates)
    ]
    for copy in to_mates:
        copy.start()
    for g in range(groups):
        fill_bias(picked_ref[g], per_group, chunk_tokens, bias_ref.at[g], own_bias_ref.at[g])
    to_scalars.wait()
    loads[3].wait()
    loads[4].wait()

    def run(steps):
        for name, *args in steps:
            {
                "z": z_step, "y": y_step, "end": gather_end, "pool": fill_pool,
                "start": return_start, "column": return_column,
                "own": return_own, "done": return_end,
            }[name](*args)

    K0, V0, K1, V1 = range(4) if groups == 2 else (0, 1, None, None)

    def stage(body, plan):
        @pl.loop(0, chunks)
        def _(c):
            body(c)
            for i, steps in enumerate(plan):
                @pl.when(c == min(i, chunks - 1))
                def _():
                    run(steps)

    def heads(g):
        return slice(g * per_group, (g + 1) * per_group)

    def between(plan):
        return lambda t: run(plan[t] if t < len(plan) else [])

    def weigh_stage(g, plan):
        work = Weigh(
            heads(g), chunk_tokens, bias_ref.at[g], own_bias_ref.at[g], q_ref, do_ref,
            pool.at[2 * g], s_ref, e_ref, acc.at[2 * g + 1],
        )
        pipelined([work.scores, work.exponents, work.products], chunks, between(plan))

    def slope_stage(g, plan):
        work = Slope(
            heads(g), chunk_tokens, q_ref, do_ref, pool.at[2 * g + 1], s_ref, e_ref,
            ds_ref.at[g], acc.at[2 * g],
        )
        pipelined([work.scores, work.products], chunks, between(plan))

    def query_stage(g, plan):
        keys_t = pool[2 * g].T
        stage(lambda c: query_grad(c, heads(g), chunk_tokens, keys_t, ds_ref.at[g], dq_ref), plan)

    run([("y", K0, 0), ("z", K0, 0), ("z", K0, 1), ("z", K0, 2), ("y", V0, 0)])
    for copy in to_mates:
        copy.wait_recv()
    backs = [
        pltpu.make_async_copy(mate_tab_ref.at[m], mate_tabs[m], in_sem.at[6 + m])
        for m in range(len(mates))
    ]
    for copy in backs:
        copy.start()
    run([("y", K1, 0), ("y", V1, 0), ("z", V0, 0), ("z", V0, 1), ("z", V0, 2), ("z", K1, 0),
         ("z", V1, 0), ("y", K0, 1), ("y", K0, 2), ("y", K0, 3), ("end", K0), ("pool", K0)])
    for copy in backs:
        copy.wait()
    weigh_stage(0, [
        [("z", K1, 1), ("y", V0, 1)],
        [("z", V1, 1), ("y", V0, 2)],
        [("y", V0, 3)],
        [("z", K1, 2), ("y", K1, 1)],
        [("z", V1, 2), ("y", V1, 1)],
    ])
    run([("start", V0), ("end", V0), ("pool", V0)])
    slope_stage(0, [
        [],
        [("y", K1, 2)],
        [("y", V1, 2)],
        [("y", K1, 3)],
    ])
    run([("start", K0), ("end", K1), ("pool", K1)])
    weigh_stage(1, [
        [],
        [("y", V1, 3)],
        [("column", V0, 0), ("column", V0, 1), ("column", V0, 2)],
        [("own", V0)],
        [("column", K0, 0), ("column", K0, 1), ("column", K0, 2)],
    ])
    run([("start", V1), ("own", K0), ("end", V1), ("pool", V1)])
    slope_stage(1, [])
    run([("start", K1)])
    query_stage(0, [
        [],
        [],
        [],
        [("column", V1, 0), ("column", V1, 1), ("column", V1, 2)],
    ])
    query_stage(1, [
        [],
        [("done", V0)],
        [("own", V1)],
        [("column", K1, 0)],
    ])
    run([("column", K1, 1), ("column", K1, 2), ("done", K0), ("own", K1), ("done", V1), ("done", K1)])
    for copy in to_mates:
        copy.wait_send()
    for p in range(pieces):
        gather_drain(p)
        return_drain(p)
    key_out[...] = mix_ref[0, : own_rows * groups].astype(jnp.bfloat16)
    value_out[...] = mix_ref[1, : own_rows * groups].astype(jnp.bfloat16)


def store_kernel(*refs):
    count = (len(refs) - 1) // 2
    sem = refs[-1]
    copies = [
        pltpu.make_async_copy(refs[i], refs[count + i], sem.at[i]) for i in range(count)
    ]
    for copy in copies:
        copy.start()
    for copy in copies:
        copy.wait()


def store(arrays):
    return pl.pallas_call(
        store_kernel,
        out_shape=tuple(jax.ShapeDtypeStruct(a.shape, a.dtype) for a in arrays),
        in_specs=[pl.BlockSpec(memory_space=pltpu.VMEM)] * len(arrays),
        out_specs=(pl.BlockSpec(memory_space=pl.ANY),) * len(arrays),
        scratch_shapes=[pltpu.SemaphoreType.DMA((len(arrays),))],
    )(*arrays)


def columns_of(mesh, n):
    spots = [getattr(d, "coords", None) for d in mesh.devices.reshape(-1, n)[0]]
    if None in spots or n % 2:
        return 1
    cols = sum(spot[2] == spots[0][2] for spot in spots) // 2
    return 2 if cols == 2 and n % 4 == 0 else 1


def local(cols, queries, keys, values, grad_out, selected):
    tokens, head_count, dh = queries.shape
    groups = keys.shape[1]
    own_blocks = tokens // BLK
    n = lax.axis_size("ctx")
    depth = n // (2 * cols)
    chips = n // 2
    pieces = 2 * groups
    fetched = min(n - 2, max(selected.shape[2] - own_blocks, 4)) + 1
    slots = -(-(own_blocks + fetched) // 16) * 16
    far_rows = -(-fetched // 8) * 8
    pool_blocks = own_blocks + fetched
    pool_rows = pool_blocks * BLK
    chunk_tokens = min(tokens, 32)
    chunks = tokens // chunk_tokens
    rows = chunk_tokens * head_count // groups
    chosen = selected.transpose(1, 2, 0)
    mates = 3 if cols > 1 else 1
    any_spec = pl.BlockSpec(memory_space=pl.ANY)
    vmem = pl.BlockSpec(memory_space=pltpu.VMEM)
    dma = pltpu.SemaphoreType.DMA
    bf16, f32, i32 = jnp.bfloat16, jnp.float32, jnp.int32
    held = pl.pallas_call(
        functools.partial(fused_kernel, n, cols, fetched, chunk_tokens, groups),
        out_shape=(
            pltpu.VMEM(queries.shape, bf16),
            pltpu.VMEM((tokens * groups, dh), bf16),
            pltpu.VMEM((tokens * groups, dh), bf16),
        ),
        in_specs=[any_spec] * 5,
        out_specs=(vmem, vmem, vmem),
        scratch_shapes=[
            pltpu.VMEM(chosen.shape, i32),
            pltpu.VMEM(queries.shape, bf16),
            pltpu.VMEM(queries.shape, bf16),
            pltpu.VMEM((2, tokens * groups, dh), bf16),
            pltpu.VMEM((2, tokens * groups + 8, dh), f32),
            pltpu.VMEM((pieces, own_blocks, BLK, dh), bf16),
            pltpu.VMEM((pieces, pool_rows, dh), bf16),
            pltpu.VMEM((pieces, pool_blocks, BLK, dh), f32),
            pltpu.VMEM((2, pool_rows, rows), f32),
            pltpu.VMEM((chunks, pool_rows, rows), f32),
            pltpu.VMEM((groups, chunks, slots, rows), f32),
            pltpu.VMEM((groups, chunks, tokens, rows), f32),
            pltpu.VMEM((groups, chunks, pool_rows, rows), bf16),
            pltpu.VMEM((groups, slots, tokens), bf16),
            pltpu.VMEM((groups, n + far_rows, LANES), i32),
            pltpu.VMEM((mates, groups, n + far_rows, LANES), i32),
            pltpu.SMEM((groups, n + far_rows, LANES), i32),
            pltpu.VMEM((pieces, mates, depth, BLK, dh), bf16),
            pltpu.VMEM((pieces, mates, depth, BLK, dh), bf16),
            pltpu.VMEM((pieces, depth, own_blocks, BLK, dh), bf16),
            pltpu.VMEM((pieces, depth, own_blocks, BLK, dh), bf16),
            pltpu.VMEM((pieces, own_blocks, BLK, dh), f32),
            dma((6 + mates,)),
            dma((2, mates)),
            dma((pieces,)),
            dma((pieces, depth)),
            dma((pieces,)),
            dma((pieces, depth)),
            dma((pieces,)),
            dma((pieces,)),
            dma((pieces, mates)),
            dma((pieces, mates, depth)),
            dma((pieces,)),
            dma((pieces,)),
        ] + [pltpu.VMEM((2, chips, own_blocks, BLK, dh), bf16)] * pieces + [pltpu.SMEM((groups, n + far_rows, LANES), i32)] * mates,
        compiler_params=pltpu.CompilerParams(collective_id=0, has_side_effects=True),
    )(
        chosen,
        queries,
        grad_out,
        keys.reshape(tokens * groups, dh),
        values.reshape(tokens * groups, dh),
    )
    held = [pltpu.with_memory_space_constraint(a, pltpu.VMEM) for a in held]
    dq, key_grad, value_grad = store(held)
    return dq, key_grad.reshape(keys.shape), value_grad.reshape(values.shape)


def solution(mesh):
    spec = P(("rep", "ctx"), None, None)
    cols = columns_of(mesh, mesh.shape["ctx"])
    return jax.shard_map(
        functools.partial(local, cols),
        mesh=mesh,
        in_specs=(spec,) * 5,
        out_specs=(spec,) * 3,
        check_vma=False,
    )
```

time: 51.4 us -> 42.1 us (0.82)
  Pallas kernels: 50.6 us -> 41.3 us
    pallas_call x1, Pallas kernels: 49.6 us -> 40.3 us  [local(): pl.pallas_call(functools.partial(fused_kernel, n, cols, fetched, chunk_to...]
where the time goes in v2:
time: 42.1 us; the launch traced here: 41.9 us
  Pallas kernels  41.3 us (98%)
  between operations  0.64 us (2%)
    pallas_call x1, Pallas kernels, local(): pl.pallas_call(functools.partial(fused_kernel, n, cols, fetched, chunk_to...  40.3 us
    pallas_call x1, Pallas kernels, store(): pl.pallas_call(store_kernel, out_shape=tuple((jax.ShapeDtypeStruct(a.shap...  1.02 us

profile of v2, /device:TPU:0, one launch (start us, length us, event | category | flops | bytes accessed | tf_op | source)
XLA Modules:
  0.0 41.9 jit_solution(9834816818080798223)
XLA Ops:
  0.6 40.3 %shard_map.76 = (bf16[128,32,128]{2,1,0:T(8,128)(2,1)S(1)}, bf16[256,128]{1,0:T(8,128)(2,1)S(1)}, bf16[256,128]{1,0:T(8,128)(2,1)S(1)}) custom-call(s32[2,8,128]{2,1,0:T(8,128)} %bitcast.7, bf16[128,32,128]{2,1,0:T(8,128)(2,1)} %q_hbm.1, bf16[128,32,128]{2,1,0:T(8,128)(2,1)} %do_hbm.1, bf16[256,128]{1,0:T(8,128)(2,1)} %bitcast.5, bf16[256,128]{1,0:T(8,128)(2,1)} %bitcast.6), custom_call_target="tpu_custom_call" | custom-call | tf_op jit(solution)/shard_map/pallas_call | solution.py:661
  40.9 1.0 %shard_map.77 = (bf16[128,32,128]{2,1,0:T(8,128)(2,1)}, bf16[256,128]{1,0:T(8,128)(2,1)}, bf16[256,128]{1,0:T(8,128)(2,1)}) custom-call(bf16[128,32,128]{2,1,0:T(8,128)(2,1)S(1)} %get-tuple-element.9.refs_0_, bf16[256,128]{1,0:T(8,128)(2,1)S(1)} %get-tuple-element.10.refs_1_, bf16[256,128]{1,0:T(8,128)(2,1)S(1)} %get-tuple-element.11.refs_2_), custom_call_target="tpu_custom_call" | custom-call | tf_op jit(solution)/shard_map/pallas_call | solution.py:622

commit v3 on v2

--- a/solution.py
+++ b/solution.py
@@ -22,8 +22,8 @@
     return part.reshape(part.shape[0] * part.shape[1], part.shape[2])
 
 
-def bands(total):
-    step = BLK * BAND
+def bands(total, band=BAND):
+    step = BLK * band
     return [(lo, min(lo + step, total)) for lo in range(0, total, step)]
 
 
@@ -107,7 +107,7 @@
     def scores(self, c):
         do = rows_of(self.do_ref, c, self.chunk_tokens, self.heads)
         total = None
-        for lo, hi in bands(self.values.shape[0]):
+        for lo, hi in bands(self.values.shape[0], 5):
             dp = lax.dot_general(self.values[lo:hi], do, NT, preferred_element_type=jnp.float32)
             for j in range(lo // BLK, hi // BLK):
                 part = dp[j * BLK - lo : (j + 1) * BLK - lo]
@@ -119,7 +119,7 @@
 
     def products(self, c):
         q = rows_of(self.q_ref, c, self.chunk_tokens, self.heads)
-        for lo, hi in bands(self.values.shape[0]):
+        for lo, hi in bands(self.values.shape[0], 5):
             dp = self.s_ref[c % 2, lo:hi]
             ds = (self.e_ref[c, lo:hi] * (dp - self.inner[c])).astype(jnp.bfloat16)
             self.ds_ref[c, lo:hi] = ds
@@ -207,10 +207,10 @@
     n, cols, n_far, chunk_tokens, groups,
     sel_hbm, q_hbm, do_hbm, k_hbm, v_hbm, dq_ref, key_out, value_out,
     sel_ref, q_ref, do_ref, raw_ref, mix_ref, own, pool, acc, s_ref, e_ref, bias_ref, own_bias_ref, ds_ref,
-    picked_ref, tab_ref, mate_tab_ref, tab, box, box_in, z_box, z_in, total_ref,
-    in_sem, tab_sem, zs, zr, ys, yr, ss, sr, box_send, box_recv, rz_send, rz_recv, *banks,
+    picked_ref, tab_ref, mate_tab_ref, tab, mate_tab, box, box_in, z_box, z_in, total_ref,
+    in_sem, done, tab_sem, zr, yr, sr, box_recv, rz_recv, *banks,
 ):
-    gaths, mate_tabs = list(banks[: 2 * groups]), list(banks[2 * groups :])
+    gaths = list(banks)
     depth = n // (2 * cols)
     chips = n // 2
     me = lax.axis_index("ctx")
@@ -249,46 +249,42 @@
             device_id_type=pl.DeviceIdType.MESH,
         )
 
-    def direct(p):
-        return p < 2
+    def turn(k):
+        return jnp.where(core == 0, depth - k, jnp.where(k == 1, 1, depth + 1 - k))
 
     def z_send(p, src, from_z, to_z):
         dst = gaths[p].at[core, from_z * cols + y]
-        return remote(src, dst, zs.at[p], zr.at[p, from_z], device(to_z, y, core))
+        return remote(src, dst, done, zr.at[p, from_z], device(to_z, y, core))
 
     def z_wait(p, from_z):
         spot = gaths[p].at[core, from_z * cols + y]
-        remote(spot, spot, zs.at[p], zr.at[p, from_z], y_peer if cols > 1 else sib).wait_recv()
+        remote(spot, spot, done, zr.at[p, from_z], y_peer if cols > 1 else sib).wait_recv()
 
     def y_send(p, src, from_z):
         dst = gaths[p].at[core, from_z * cols + y]
-        return remote(src, dst, ys.at[p], yr.at[p, from_z], y_peer)
+        return remote(src, dst, done, yr.at[p, from_z], y_peer)
 
     def y_wait(p, from_z):
         spot = gaths[p].at[core, from_z * cols + other_y]
-        remote(spot, spot, ys.at[p], yr.at[p, from_z], y_peer).wait_recv()
+        remote(spot, spot, done, yr.at[p, from_z], y_peer).wait_recv()
 
     def sib_send(p, src, q):
-        return remote(src, gaths[p].at[core, q], ss.at[p], sr.at[p], sib)
+        return remote(src, gaths[p].at[core, q], done, sr.at[p], sib)
 
     def gather_start(p):
         if cols > 1:
             y_send(p, own.at[p], z).start()
 
-        if direct(p):
-            @pl.loop(1, depth)
-            def _(k):
-                z_send(p, own.at[p], z, near(depth - k)).start()
-        else:
-            for to_z in (z - 1, z + 1):
-                @pl.when((to_z >= 0) & (to_z < depth))
-                def _():
-                    z_send(p, own.at[p], z, to_z).start()
+        @pl.loop(1, depth)
+        def _(k):
+            z_send(p, own.at[p], z, near(turn(k))).start()
 
         sib_send(p, own.at[p], chip).start()
 
     def span(i):
         return 1 + i * near_max // 3, 1 + (i + 1) * near_max // 3
+
+    pair = z + 1 - 2 * lax.rem(z, 2)
 
     def each_at(d, visit):
         for side in (-1, 1):
@@ -296,23 +292,21 @@
 
             @pl.when((from_z >= 0) & (from_z < depth))
             def _():
-                visit(from_z, z - side)
+                visit(from_z)
 
     def z_step(p, i):
         lo, hi = span(i)
 
-        def visit(from_z, to_z):
+        def visit(from_z):
             q = from_z * cols + y
             spot = gaths[p].at[core, q]
             z_wait(p, from_z)
-            if not direct(p):
-                @pl.when((to_z >= 0) & (to_z < depth))
+
+            if cols > 1:
+                @pl.when((core == 1) | (from_z != pair) | (pair >= depth))
                 def _():
-                    z_send(p, spot, from_z, to_z).start()
-
-
-            if cols > 1:
-                y_send(p, spot, from_z).start()
+                    y_send(p, spot, from_z).start()
+
             sib_send(p, spot, q).start()
 
         @pl.loop(lo, hi)
@@ -323,13 +317,19 @@
         if cols == 1:
             return
 
-        def visit(from_z, to_z):
+        def visit(from_z):
             q = from_z * cols + other_y
+            spot = gaths[p].at[core, q]
             y_wait(p, from_z)
-            sib_send(p, gaths[p].at[core, q], q).start()
+            if i == 0:
+                @pl.when((core == 0) & (pair < depth))
+                def _():
+                    remote(spot, spot, done, yr.at[p, z], device(pair, y, core)).start()
+
+            sib_send(p, spot, q).start()
 
         if i == 0:
-            visit(z, z)
+            visit(z)
         else:
             lo, hi = span(i - 1)
 
@@ -339,27 +339,16 @@
 
     def gather_end(p):
         spot = gaths[p].at[1 - core]
-        remote(spot, spot, ss.at[p], sr.at[p], sib).wait_recv()
-
-    def z_drain(p, count):
-        @pl.loop(0, count)
-        def _(k):
-            z_send(p, own.at[p], z, z).wait_send()
+        remote(spot, spot, done, sr.at[p], sib).wait_recv()
 
     def gather_drain(p):
         spot = gaths[p].at[core]
-        remote(spot, spot, ss.at[p], sr.at[p], sib).wait_send()
-        if direct(p):
-            z_drain(p, depth - 1)
-        else:
-            for more, count in ((z > 0, depth - z), (z < depth - 1, z + 1)):
-                @pl.when(more)
-                def _():
-                    z_drain(p, count)
-
+        remote(spot, spot, done, sr.at[p], sib).wait_send()
+        part = gaths[p].at[core, pl.ds(0, depth - 1)]
+        remote(part, part, done, zr.at[p, z], sib).wait_send()
         if cols > 1:
             part = gaths[p].at[core, pl.ds(0, depth)]
-            remote(part, part, ys.at[p], yr.at[p, z], y_peer).wait_send()
+            remote(part, part, done, yr.at[p, z], y_peer).wait_send()
 
     def fill_pool(p):
         g = p // 2
@@ -374,13 +363,13 @@
 
     def mate_copy(p, m, zz):
         return remote(
-            box.at[p, m, zz], box_in.at[p, m, zz], box_send.at[p, m], box_recv.at[p, m, zz],
+            box.at[p, zz, m], box_in.at[p, zz, m], done, box_recv.at[p, zz],
             device(z, *mates[m]),
         )
 
     def z_copy(p, to_z):
         return remote(
-            z_box.at[p, to_z], z_in.at[p, z], rz_send.at[p], rz_recv.at[p], device(to_z, y, core)
+            z_box.at[p, to_z], z_in.at[p, z], done, rz_recv.at[p], device(to_z, y, core)
         )
 
     def factor(p):
@@ -401,19 +390,19 @@
             for m, (yy, cc) in enumerate(mates):
                 dest = device(zz, yy, cc)
                 keep = tab[g, dest, 1].astype(jnp.float32) * factor(p)
-                box[p, m, zz] = (far_part(p, dest) * keep).astype(jnp.bfloat16)
+                box[p, zz, m] = (far_part(p, dest) * keep).astype(jnp.bfloat16)
             for m in range(len(mates)):
                 mate_copy(p, m, zz).start()
 
     def merged(p, zz):
         g = p // 2
         dest = device(zz, y, core)
+        spot = box_in.at[p, zz]
+        remote(spot, spot, done, box_recv.at[p, zz], sib).wait_recv()
+        parts = [far_part(p, dest) * (tab[g, dest, 1].astype(jnp.float32) * factor(p))]
+        tables = [tab] + [mate_tab.at[m] for m in range(len(mates))]
         for m in range(len(mates)):
-            mate_copy(p, m, zz).wait_recv()
-        parts = [far_part(p, dest) * (tab[g, dest, 1].astype(jnp.float32) * factor(p))]
-        tables = [tab] + mate_tabs
-        for m in range(len(mates)):
-            parts.append(box_in[p, m, zz].astype(jnp.float32))
+            parts.append(box_in[p, zz, m].astype(jnp.float32))
         for b in range(own_blocks):
             total = None
             for table, part in zip(tables, parts):
@@ -437,7 +426,7 @@
 
     def return_end(p):
         part = z_in.at[p, pl.ds(0, depth - 1)]
-        remote(part, part, rz_send.at[p], rz_recv.at[p], sib).wait_recv()
+        remote(part, part, done, rz_recv.at[p], sib).wait_recv()
 
         @pl.loop(1, depth)
         def _(k):
@@ -448,11 +437,10 @@
         mix_ref[p % 2, pl.ds(p // 2, own_rows, stride=groups), :] = whole
 
     def return_drain(p):
-        for m in range(len(mates)):
-            part = box.at[p, m]
-            remote(part, part, box_send.at[p, m], box_recv.at[p, m, 0], sib).wait_send()
+        part = box.at[p]
+        remote(part, part, done, box_recv.at[p, 0], sib).wait_send()
         part = z_box.at[p, pl.ds(0, depth - 1)]
-        remote(part, part, rz_send.at[p], rz_recv.at[p], sib).wait_send()
+        remote(part, part, done, rz_recv.at[p], sib).wait_send()
 
     barrier = pltpu.get_barrier_semaphore()
 
@@ -467,41 +455,44 @@
 
     for yy, cc in mates:
         greet(device(z, yy, cc))
-    loads = [
-        pltpu.make_async_copy(src, dst, in_sem.at[i])
-        for i, (src, dst) in enumerate([
-            (k_hbm, raw_ref.at[0]), (v_hbm, raw_ref.at[1]), (sel_hbm, sel_ref), (q_hbm, q_ref), (do_hbm, do_ref),
-        ])
+    kv_loads = [
+        pltpu.make_async_copy(k_hbm, raw_ref.at[0], in_sem.at[0]),
+        pltpu.make_async_copy(v_hbm, raw_ref.at[1], in_sem.at[1]),
     ]
-    for load in loads:
+    sel_load = pltpu.make_async_copy(sel_hbm, sel_ref, in_sem.at[2])
+    rest = [
+        pltpu.make_async_copy(q_hbm, q_ref, in_sem.at[3]),
+        pltpu.make_async_copy(do_hbm, do_ref, in_sem.at[4]),
+    ]
+    for load in kv_loads + [sel_load] + rest:
         load.start()
     for kv in range(2):
-        loads[kv].wait()
+        kv_loads[kv].wait()
         mix_ref[kv, : own_rows * groups] = raw_ref[kv].astype(jnp.float32)
         for g in range(groups):
             rows = mix_ref[kv, pl.ds(g, own_rows, stride=groups), :].astype(jnp.bfloat16)
             own[2 * g + kv] = rows.reshape(own_blocks, BLK, dh)
     pl.semaphore_wait(barrier, depth - 1 + len(mates))
-    for p in range(pieces):
-        gather_start(p)
-    loads[2].wait()
+    gather_start(0)
+    sel_load.wait()
     for g in range(groups):
         fill_tables(g, n, me, n_far, own_blocks, sel_ref, picked_ref, tab_ref)
-    to_scalars = pltpu.make_async_copy(tab_ref, tab, in_sem.at[5])
+    to_scalars = pltpu.make_async_copy(tab_ref, tab, in_sem.at[2])
     to_scalars.start()
     to_mates = [
         remote(
-            tab_ref, mate_tab_ref.at[m], tab_sem.at[0, m], tab_sem.at[1, m], device(z, yy, cc)
+            tab_ref, mate_tab_ref.at[m], done, tab_sem, device(z, yy, cc)
         )
         for m, (yy, cc) in enumerate(mates)
     ]
     for copy in to_mates:
         copy.start()
+    gather_start(1)
     for g in range(groups):
         fill_bias(picked_ref[g], per_group, chunk_tokens, bias_ref.at[g], own_bias_ref.at[g])
     to_scalars.wait()
-    loads[3].wait()
-    loads[4].wait()
+    for load in rest:
+        load.wait()
 
     def run(steps):
         for name, *args in steps:
@@ -546,59 +537,61 @@
         keys_t = pool[2 * g].T
         stage(lambda c: query_grad(c, heads(g), chunk_tokens, keys_t, ds_ref.at[g], dq_ref), plan)
 
+    for p in range(2, pieces):
+        gather_start(p)
     run([("y", K0, 0), ("z", K0, 0), ("z", K0, 1), ("z", K0, 2), ("y", V0, 0)])
-    for copy in to_mates:
-        copy.wait_recv()
-    backs = [
-        pltpu.make_async_copy(mate_tab_ref.at[m], mate_tabs[m], in_sem.at[6 + m])
-        for m in range(len(mates))
-    ]
-    for copy in backs:
-        copy.start()
-    run([("y", K1, 0), ("y", V1, 0), ("z", V0, 0), ("z", V0, 1), ("z", V0, 2), ("z", K1, 0),
-         ("z", V1, 0), ("y", K0, 1), ("y", K0, 2), ("y", K0, 3), ("end", K0), ("pool", K0)])
-    for copy in backs:
-        copy.wait()
+    remote(mate_tab_ref, mate_tab_ref, done, tab_sem, sib).wait_recv()
+    back = pltpu.make_async_copy(mate_tab_ref, mate_tab, in_sem.at[3])
+    back.start()
+    run([("y", K1, 0), ("y", V1, 0), ("z", V0, 0), ("z", V0, 1), ("z", V0, 2), ("y", K0, 1),
+         ("y", K0, 2), ("y", K0, 3), ("end", K0), ("pool", K0)])
+    back.wait()
     weigh_stage(0, [
-        [("z", K1, 1), ("y", V0, 1)],
-        [("z", V1, 1), ("y", V0, 2)],
-        [("y", V0, 3)],
-        [("z", K1, 2), ("y", K1, 1)],
-        [("z", V1, 2), ("y", V1, 1)],
+        [],
+        [("z", K1, 0)],
+        [("y", V0, 1)],
+        [("z", K1, 1)],
+        [("y", V0, 2), ("z", K1, 2)],
+        [("y", V0, 3), ("z", V1, 0)],
     ])
-    run([("start", V0), ("end", V0), ("pool", V0)])
+    run([("z", V1, 1), ("end", V0), ("pool", V0)])
     slope_stage(0, [
+        [("z", V1, 2), ("y", K1, 1)],
         [],
-        [("y", K1, 2)],
-        [("y", V1, 2)],
+        [("start", V0), ("y", K1, 2)],
         [("y", K1, 3)],
     ])
-    run([("start", K0), ("end", K1), ("pool", K1)])
+    run([("start", K0), ("y", V1, 1), ("end", K1), ("pool", K1)])
     weigh_stage(1, [
         [],
+        [("y", V1, 2)],
+        [],
         [("y", V1, 3)],
-        [("column", V0, 0), ("column", V0, 1), ("column", V0, 2)],
-        [("own", V0)],
-        [("column", K0, 0), ("column", K0, 1), ("column", K0, 2)],
+        [("column", V0, 0)],
+        [("column", V0, 1)],
     ])
-    run([("start", V1), ("own", K0), ("end", V1), ("pool", V1)])
-    slope_stage(1, [])
-    run([("start", K1)])
+    run([("start", V1), ("end", V1), ("pool", V1)])
+    slope_stage(1, [
+        [("column", V0, 2)],
+        [("column", K0, 0)],
+        [("column", K0, 1)],
+        [("column", K0, 2)],
+    ])
+    run([("start", K1), ("own", V0), ("own", K0)])
     query_stage(0, [
-        [],
-        [],
-        [],
-        [("column", V1, 0), ("column", V1, 1), ("column", V1, 2)],
+        [("column", V1, 0)],
+        [("column", V1, 1)],
+        [("column", V1, 2)],
+        [("done", V0)],
     ])
     query_stage(1, [
         [],
-        [("done", V0)],
-        [("own", V1)],
-        [("column", K1, 0)],
+        [("own", V1), ("column", K1, 0), ("column", K1, 1), ("column", K1, 2)],
+        [("own", K1)],
+        [("done", K0), ("done", V1)],
     ])
-    run([("column", K1, 1), ("column", K1, 2), ("done", K0), ("own", K1), ("done", V1), ("done", K1)])
-    for copy in to_mates:
-        copy.wait_send()
+    run([("done", K1)])
+    remote(mate_tab_ref, mate_tab_ref, done, tab_sem, sib).wait_send()
     for p in range(pieces):
         gather_drain(p)
         return_drain(p)
@@ -685,24 +678,21 @@
             pltpu.VMEM((groups, n + far_rows, LANES), i32),
             pltpu.VMEM((mates, groups, n + far_rows, LANES), i32),
             pltpu.SMEM((groups, n + far_rows, LANES), i32),
-            pltpu.VMEM((pieces, mates, depth, BLK, dh), bf16),
-            pltpu.VMEM((pieces, mates, depth, BLK, dh), bf16),
+            pltpu.SMEM((mates, groups, n + far_rows, LANES), i32),
+            pltpu.VMEM((pieces, depth, mates, BLK, dh), bf16),
+            pltpu.VMEM((pieces, depth, mates, BLK, dh), bf16),
             pltpu.VMEM((pieces, depth, own_blocks, BLK, dh), bf16),
             pltpu.VMEM((pieces, depth, own_blocks, BLK, dh), bf16),
             pltpu.VMEM((pieces, own_blocks, BLK, dh), f32),
-            dma((6 + mates,)),
-            dma((2, mates)),
-            dma((pieces,)),
+            dma((5,)),
+            dma,
+            dma,
+            dma((pieces, depth)),
             dma((pieces, depth)),
             dma((pieces,)),
             dma((pieces, depth)),
             dma((pieces,)),
-            dma((pieces,)),
-            dma((pieces, mates)),
-            dma((pieces, mates, depth)),
-            dma((pieces,)),
-            dma((pieces,)),
-        ] + [pltpu.VMEM((2, chips, own_blocks, BLK, dh), bf16)] * pieces + [pltpu.SMEM((groups, n + far_rows, LANES), i32)] * mates,
+        ] + [pltpu.VMEM((2, chips, own_blocks, BLK, dh), bf16)] * pieces,
         compiler_params=pltpu.CompilerParams(collective_id=0, has_side_effects=True),
     )(
         chosen,

time: 42.1 us -> 41.4 us (0.983)
  Pallas kernels: 41.3 us -> 40.6 us
    pallas_call x1, Pallas kernels: 40.3 us -> 39.6 us  [local(): pl.pallas_call(functools.partial(fused_kernel, n, cols, fetched, chunk_to...]
where the time goes in v3:
time: 41.4 us; the launch traced here: 41.3 us
  Pallas kernels  40.6 us (98%)
  between operations  0.64 us (2%)
    pallas_call x1, Pallas kernels, local(): pl.pallas_call(functools.partial(fused_kernel, n, cols, fetched, chunk_to...  39.6 us
    pallas_call x1, Pallas kernels, store(): pl.pallas_call(store_kernel, out_shape=tuple((jax.ShapeDtypeStruct(a.shap...  1.02 us

profile of v3, /device:TPU:0, one launch (start us, length us, event | category | flops | bytes accessed | tf_op | source)
XLA Modules:
  0.0 41.3 jit_solution(2185302880611675712)
XLA Ops:
  0.6 39.6 %shard_map.76 = (bf16[128,32,128]{2,1,0:T(8,128)(2,1)S(1)}, bf16[256,128]{1,0:T(8,128)(2,1)S(1)}, bf16[256,128]{1,0:T(8,128)(2,1)S(1)}) custom-call(s32[2,8,128]{2,1,0:T(8,128)} %bitcast.7, bf16[128,32,128]{2,1,0:T(8,128)(2,1)} %q_hbm.1, bf16[128,32,128]{2,1,0:T(8,128)(2,1)} %do_hbm.1, bf16[256,128]{1,0:T(8,128)(2,1)} %bitcast.5, bf16[256,128]{1,0:T(8,128)(2,1)} %bitcast.6), custom_call_target="tpu_custom_call" | custom-call | tf_op jit(solution)/shard_map/pallas_call | solution.py:654
  40.2 1.0 %shard_map.77 = (bf16[128,32,128]{2,1,0:T(8,128)(2,1)}, bf16[256,128]{1,0:T(8,128)(2,1)}, bf16[256,128]{1,0:T(8,128)(2,1)}) custom-call(bf16[128,32,128]{2,1,0:T(8,128)(2,1)S(1)} %get-tuple-element.9.refs_0_, bf16[256,128]{1,0:T(8,128)(2,1)S(1)} %get-tuple-element.10.refs_1_, bf16[256,128]{1,0:T(8,128)(2,1)S(1)} %get-tuple-element.11.refs_2_), custom_call_target="tpu_custom_call" | custom-call | tf_op jit(solution)/shard_map/pallas_call | solution.py:615

commit v4 on v3

--- a/solution.py
+++ b/solution.py
@@ -22,53 +22,62 @@
     return part.reshape(part.shape[0] * part.shape[1], part.shape[2])
 
 
-def bands(total, band=BAND):
-    step = BLK * band
-    return [(lo, min(lo + step, total)) for lo in range(0, total, step)]
+def bands(total, start=0):
+    step = BLK * BAND
+    return [(lo, min(lo + step, total)) for lo in range(start, total, step)]
 
 
 def fold(x, op):
     return op(x.reshape(x.shape[0] // 8, 8, x.shape[1]), axis=0)
 
 
-def fill_bias(picked, per_group, chunk_tokens, bias_ref, own_bias_ref):
-    tokens = picked.shape[1]
+def fill_own(g, per_group, chunk_tokens, picked, q_ref, do_ref, own, bias_ref, score_ref, peak_ref, slope_ref):
+    tokens, dh = picked.shape[1], own.shape[3]
     rows = chunk_tokens * per_group
     shift = per_group.bit_length() - 1
+    heads = slice(g * per_group, (g + 1) * per_group)
 
     @pl.loop(0, tokens // chunk_tokens)
     def _(c):
-        row_tok = c * chunk_tokens + (lax.broadcasted_iota(jnp.int32, (tokens, rows), 1) >> shift)
+        t0 = pl.multiple_of(c * chunk_tokens, chunk_tokens)
+        q = q_ref[pl.ds(t0, chunk_tokens), heads, :].reshape(rows, dh)
+        do = do_ref[pl.ds(t0, chunk_tokens), heads, :].reshape(rows, dh)
+        row_tok = t0 + (lax.broadcasted_iota(jnp.int32, (tokens, rows), 1) >> shift)
         tok = lax.broadcasted_iota(jnp.int32, (tokens, rows), 0)
         spread = jnp.where(row_tok == tok, 1.0, 0.0).astype(jnp.bfloat16)
         seen = lax.dot_general(picked, spread, NN, preferred_element_type=jnp.float32)
         bias = (seen - 1.0) * (-NEG)
         bias_ref[c] = bias
+        keys, values = own[2 * g].reshape(tokens, dh), own[2 * g + 1].reshape(tokens, dh)
+        s = lax.dot_general(keys, q, NT, preferred_element_type=jnp.float32)
+        slope_ref[c] = lax.dot_general(values, do, NT, preferred_element_type=jnp.float32)
+        peak = None
         for j in range(tokens // BLK):
             at = slice(j * BLK, (j + 1) * BLK)
-            own_bias_ref[c, at] = jnp.where(tok[at] <= row_tok[at], bias[j : j + 1], NEG)
+            part = jnp.where(tok[at] <= row_tok[at], s[at] + bias[j : j + 1], NEG)
+            score_ref[c, at] = part
+            top = fold(part, jnp.max)
+            peak = top if peak is None else jnp.maximum(peak, top)
+        peak_ref[c] = peak
 
 
 class Weigh:
-    def __init__(self, heads, chunk_tokens, bias, own_bias, q_ref, do_ref, keys, s_ref, e_ref, acc_ref):
+    def __init__(self, heads, chunk_tokens, bias, own_score, own_peak, q_ref, do_ref, keys, s_ref, e_ref, acc_ref):
         self.__dict__.update(locals())
         self.peak, self.inv = {}, {}
 
     def scores(self, c):
         tokens, _, dh = self.q_ref.shape
         q = rows_of(self.q_ref, c, self.chunk_tokens, self.heads)
-        peak = None
-        for lo, hi in bands(self.keys.shape[0]):
+        peak = self.own_peak[c]
+        for lo, hi in bands(self.keys.shape[0], tokens):
             s = lax.dot_general(self.keys[lo:hi], q, NT, preferred_element_type=jnp.float32)
             for j in range(lo // BLK, hi // BLK):
                 part = s[j * BLK - lo : (j + 1) * BLK - lo]
-                if j < tokens // BLK:
-                    part = part + self.own_bias[c, j * BLK : (j + 1) * BLK]
-                else:
-                    part = part + self.bias[c, j : j + 1]
+                part = part + self.bias[c, j : j + 1]
                 self.s_ref[c % 2, j * BLK : (j + 1) * BLK] = part
                 top = fold(part, jnp.max)
-                peak = top if peak is None else jnp.maximum(peak, top)
+                peak = jnp.maximum(peak, top)
             yield
         log_scale = LOG2E / math.sqrt(dh)
         self.peak[c] = jnp.max(peak, axis=0, keepdims=True) * log_scale
@@ -80,7 +89,9 @@
         for lo, hi in bands(self.keys.shape[0]):
             for j in range(lo // BLK, hi // BLK):
                 at = slice(j * BLK, (j + 1) * BLK)
-                e = jnp.exp2(self.s_ref[c % 2, at] * log_scale - self.peak[c])
+                far = j >= self.own_score.shape[1] // BLK
+                s = self.s_ref[c % 2, at] if far else self.own_score[c, at]
+                e = jnp.exp2(s * log_scale - self.peak[c])
                 self.e_ref[c, at] = e
                 part = fold(e, jnp.sum)
                 total = part if total is None else total + part
@@ -100,27 +111,29 @@
 
 
 class Slope:
-    def __init__(self, heads, chunk_tokens, q_ref, do_ref, values, s_ref, e_ref, ds_ref, acc_ref):
+    def __init__(self, heads, chunk_tokens, own_slope, q_ref, do_ref, values, s_ref, e_ref, ds_ref, acc_ref):
         self.__dict__.update(locals())
         self.inner = {}
 
     def scores(self, c):
         do = rows_of(self.do_ref, c, self.chunk_tokens, self.heads)
-        total = None
-        for lo, hi in bands(self.values.shape[0], 5):
+        own_rows = self.own_slope.shape[1]
+        total = fold(self.own_slope[c] * self.e_ref[c, :own_rows], jnp.sum)
+        for lo, hi in bands(self.values.shape[0], own_rows):
             dp = lax.dot_general(self.values[lo:hi], do, NT, preferred_element_type=jnp.float32)
             for j in range(lo // BLK, hi // BLK):
                 part = dp[j * BLK - lo : (j + 1) * BLK - lo]
                 self.s_ref[c % 2, j * BLK : (j + 1) * BLK] = part
                 part = fold(part * self.e_ref[c, j * BLK : (j + 1) * BLK], jnp.sum)
-                total = part if total is None else total + part
+                total = total + part
             yield
         self.inner[c] = jnp.sum(total, axis=0, keepdims=True)
 
     def products(self, c):
         q = rows_of(self.q_ref, c, self.chunk_tokens, self.heads)
-        for lo, hi in bands(self.values.shape[0], 5):
-            dp = self.s_ref[c % 2, lo:hi]
+        own_rows = self.own_slope.shape[1]
+        for lo, hi in [(0, own_rows)] + bands(self.values.shape[0], own_rows):
+            dp = self.s_ref[c % 2, lo:hi] if lo >= own_rows else self.own_slope[c]
             ds = (self.e_ref[c, lo:hi] * (dp - self.inner[c])).astype(jnp.bfloat16)
             self.ds_ref[c, lo:hi] = ds
             dk = lax.dot_general(ds, q, NN, preferred_element_type=jnp.float32)
@@ -206,7 +219,7 @@
 def fused_kernel(
     n, cols, n_far, chunk_tokens, groups,
     sel_hbm, q_hbm, do_hbm, k_hbm, v_hbm, dq_ref, key_out, value_out,
-    sel_ref, q_ref, do_ref, raw_ref, mix_ref, own, pool, acc, s_ref, e_ref, bias_ref, own_bias_ref, ds_ref,
+    sel_ref, q_ref, do_ref, raw_ref, mix_ref, own, pool, acc, s_ref, e_ref, bias_ref, own_score_ref, own_peak_ref, own_slope_ref, ds_ref,
     picked_ref, tab_ref, mate_tab_ref, tab, mate_tab, box, box_in, z_box, z_in, total_ref,
     in_sem, done, tab_sem, zr, yr, sr, box_recv, rz_recv, *banks,
 ):
@@ -488,11 +501,17 @@
     for copy in to_mates:
         copy.start()
     gather_start(1)
-    for g in range(groups):
-        fill_bias(picked_ref[g], per_group, chunk_tokens, bias_ref.at[g], own_bias_ref.at[g])
     to_scalars.wait()
     for load in rest:
         load.wait()
+    for g in range(groups):
+        fill_own(
+            g, per_group, chunk_tokens, picked_ref[g], q_ref, do_ref, own, bias_ref.at[g],
+            own_score_ref.at[g], own_peak_ref.at[g], own_slope_ref.at[g],
+        )
+        if g == 0:
+            for p in range(2, pieces):
+                gather_start(p)
 
     def run(steps):
         for name, *args in steps:
@@ -521,14 +540,14 @@
 
     def weigh_stage(g, plan):
         work = Weigh(
-            heads(g), chunk_tokens, bias_ref.at[g], own_bias_ref.at[g], q_ref, do_ref,
-            pool.at[2 * g], s_ref, e_ref, acc.at[2 * g + 1],
+            heads(g), chunk_tokens, bias_ref.at[g], own_score_ref.at[g], own_peak_ref.at[g],
+            q_ref, do_ref, pool.at[2 * g], s_ref, e_ref, acc.at[2 * g + 1],
         )
         pipelined([work.scores, work.exponents, work.products], chunks, between(plan))
 
     def slope_stage(g, plan):
         work = Slope(
-            heads(g), chunk_tokens, q_ref, do_ref, pool.at[2 * g + 1], s_ref, e_ref,
+            heads(g), chunk_tokens, own_slope_ref.at[g], q_ref, do_ref, pool.at[2 * g + 1], s_ref, e_ref,
             ds_ref.at[g], acc.at[2 * g],
         )
         pipelined([work.scores, work.products], chunks, between(plan))
@@ -537,8 +556,6 @@
         keys_t = pool[2 * g].T
         stage(lambda c: query_grad(c, heads(g), chunk_tokens, keys_t, ds_ref.at[g], dq_ref), plan)
 
-    for p in range(2, pieces):
-        gather_start(p)
     run([("y", K0, 0), ("z", K0, 0), ("z", K0, 1), ("z", K0, 2), ("y", V0, 0)])
     remote(mate_tab_ref, mate_tab_ref, done, tab_sem, sib).wait_recv()
     back = pltpu.make_async_copy(mate_tab_ref, mate_tab, in_sem.at[3])
@@ -549,17 +566,17 @@
     weigh_stage(0, [
         [],
         [("z", K1, 0)],
-        [("y", V0, 1)],
+        [],
         [("z", K1, 1)],
-        [("y", V0, 2), ("z", K1, 2)],
-        [("y", V0, 3), ("z", V1, 0)],
+        [("z", K1, 2), ("y", V0, 1)],
+        [("z", V1, 0), ("y", V0, 2)],
     ])
-    run([("z", V1, 1), ("end", V0), ("pool", V0)])
+    run([("z", V1, 1), ("y", V0, 3), ("end", V0), ("pool", V0)])
     slope_stage(0, [
         [("z", V1, 2), ("y", K1, 1)],
+        [("y", K1, 2)],
+        [("start", V0), ("y", K1, 3)],
         [],
-        [("start", V0), ("y", K1, 2)],
-        [("y", K1, 3)],
     ])
     run([("start", K0), ("y", V1, 1), ("end", K1), ("pool", K1)])
     weigh_stage(1, [
@@ -573,11 +590,12 @@
     run([("start", V1), ("end", V1), ("pool", V1)])
     slope_stage(1, [
         [("column", V0, 2)],
+        [],
+        [],
         [("column", K0, 0)],
         [("column", K0, 1)],
-        [("column", K0, 2)],
     ])
-    run([("start", K1), ("own", V0), ("own", K0)])
+    run([("start", K1), ("column", K0, 2), ("own", V0), ("own", K0)])
     query_stage(0, [
         [("column", V1, 0)],
         [("column", V1, 1)],
@@ -673,6 +691,8 @@
             pltpu.VMEM((chunks, pool_rows, rows), f32),
             pltpu.VMEM((groups, chunks, slots, rows), f32),
             pltpu.VMEM((groups, chunks, tokens, rows), f32),
+            pltpu.VMEM((groups, chunks, 8, rows), f32),
+            pltpu.VMEM((groups, chunks, tokens, rows), f32),
             pltpu.VMEM((groups, chunks, pool_rows, rows), bf16),
             pltpu.VMEM((groups, slots, tokens), bf16),
             pltpu.VMEM((groups, n + far_rows, LANES), i32),

time: 41.4 us -> 41 us (level)
    pallas_call x1, Pallas kernels: 39.6 us -> 39.1 us  [local(): pl.pallas_call(functools.partial(fused_kernel, n, cols, fetched, chunk_to...]
where the time goes in v4:
time: 41 us; the launch traced here: 40.8 us
  Pallas kernels  40.2 us (98%)
  between operations  0.64 us (2%)
    pallas_call x1, Pallas kernels, local(): pl.pallas_call(functools.partial(fused_kernel, n, cols, fetched, chunk_to...  39.1 us
    pallas_call x1, Pallas kernels, store(): pl.pallas_call(store_kernel, out_shape=tuple((jax.ShapeDtypeStruct(a.shap...  1.02 us

profile of v4, /device:TPU:0, one launch (start us, length us, event | category | flops | bytes accessed | tf_op | source)
XLA Modules:
  0.0 40.8 jit_solution(5248209112673096160)
XLA Ops:
  0.6 39.1 %shard_map.76 = (bf16[128,32,128]{2,1,0:T(8,128)(2,1)S(1)}, bf16[256,128]{1,0:T(8,128)(2,1)S(1)}, bf16[256,128]{1,0:T(8,128)(2,1)S(1)}) custom-call(s32[2,8,128]{2,1,0:T(8,128)} %bitcast.7, bf16[128,32,128]{2,1,0:T(8,128)(2,1)} %q_hbm.1, bf16[128,32,128]{2,1,0:T(8,128)(2,1)} %do_hbm.1, bf16[256,128]{1,0:T(8,128)(2,1)} %bitcast.5, bf16[256,128]{1,0:T(8,128)(2,1)} %bitcast.6), custom_call_target="tpu_custom_call" | custom-call | tf_op jit(solution)/shard_map/pallas_call | solution.py:672
  39.8 1.0 %shard_map.77 = (bf16[128,32,128]{2,1,0:T(8,128)(2,1)}, bf16[256,128]{1,0:T(8,128)(2,1)}, bf16[256,128]{1,0:T(8,128)(2,1)}) custom-call(bf16[128,32,128]{2,1,0:T(8,128)(2,1)S(1)} %get-tuple-element.9.refs_0_, bf16[256,128]{1,0:T(8,128)(2,1)S(1)} %get-tuple-element.10.refs_1_, bf16[256,128]{1,0:T(8,128)(2,1)S(1)} %get-tuple-element.11.refs_2_), custom_call_target="tpu_custom_call" | custom-call | tf_op jit(solution)/shard_map/pallas_call | solution.py:633
